TPU v7x, 32 devices: a whole 2x2x4 slice. The times are simulated.
32 devices in a mesh: groups: 2 (over y), fft: 4 (over z), band: 2 (over x), sub: 2 (over core).
Axes of the slice: x: 2, y: 2, z: 4, core: 2. Of those that a mesh axis runs over, the one named last changes fastest.
Arguments:
- coefficients: bfloat16 [8, 2, 128, 1024], P(('groups', 'band', 'sub'), None, None, 'fft'), parts along dimension 0, may hold values from -6 to 6
- potential: float32 [384, 192, 192], P(('groups', 'fft')), parts along dimension 0, may hold values from -15 to 15
- stick_map: int32 [3, 2048], P(None, ('groups', 'fft')), parts along dimension 1, may hold values from 0 to 191, as said below
- plane_order: int32 [384], P('groups'), parts along dimension 0, may hold values from 0 to 191, each once
Outputs:
- applied: float32 [8, 2, 128, 1024], P(('groups', 'band', 'sub'), None, None, 'fft'), parts along dimension 0
There are 2 independent parts, one for each index of `groups`. A program takes and returns all parts, laid end to end along the dimension named above; each array names one. Nothing has to cross between parts.
Inputs may be any that keep to these rules, and one draw needn't show every extreme that they name: Column s is one stick slot: stick_map[0, s] and stick_map[1, s] are its grid indices x and y, stick_map[2, s] its length, an odd number up to 127, or 0 for an empty slot. A stick of length L holds the frequencies -(L - 1)/2 to (L - 1)/2 at entries 128/2 + f. The number of live slots differs between indices of fft; some index has all 256 slots live, and 512 slots are live in all. Live sticks name distinct columns, whose frequencies (indices taken modulo 192 into -96 to 95) lie in -48 to 47 along x and along y; an empty slot may name any column. `plane_order`: each plane number appears once.
All inputs are finite; a program needn't handle non-finite values.
Results may differ from a plain program's by a relative error of at most 0.0084.
Values may be sent and summed in bfloat16 or wider, within the bound.
No kernel may reach another device: no remote copies, remote signals or barrier semaphores. Data moves between devices by JAX's collectives and lax.ppermute only.
A program may use at most 128 MiB of HBM per device.

v0:
```python
import math

import jax
import jax.numpy as jnp
from jax import lax
from jax.sharding import PartitionSpec as P


def phase_tables(left_ids, right_ids, modulus):
    turn_index = left_ids[:, None] * right_ids[None, :] % modulus
    angles = turn_index.astype(jnp.float32) * (2.0 * math.pi / modulus)
    return (jnp.cos(angles).astype(jnp.bfloat16), jnp.sin(angles).astype(jnp.bfloat16))


def row_numbers(grid_side):
    compact = jnp.arange(grid_side // 2, dtype=jnp.int32)
    return jnp.where(compact < grid_side // 4, compact, compact + grid_side // 2)


def compact_rows(grid_ids, grid_side):
    rows = jnp.where(grid_ids < grid_side // 4, grid_ids, grid_ids - grid_side // 2)
    return jnp.clip(rows, 0, grid_side // 2 - 1)


def one_hot_rows(grid_ids, grid_side):
    rows = compact_rows(grid_ids, grid_side)
    slots = jnp.arange(grid_side // 2, dtype=jnp.int32)
    return (rows[:, None] == slots[None, :]).astype(jnp.bfloat16)


def plane_work(received, x_onehot, y_onehot, sources, depth_count, grid_side, potential_rows):
    planes = received.shape[0]
    half_side = grid_side // 2
    slot_count = x_onehot.shape[0] // sources

    def place_one(row):
        values = row.reshape(sources, depth_count, 2, slot_count).transpose(1, 2, 0, 3)
        values = values.reshape(depth_count, 2, sources * slot_count)
        weighted = values[..., None] * y_onehot[None, None]
        return jnp.einsum(
            "sx,dcsy->dxcy", x_onehot, weighted, preferred_element_type=jnp.float32
        ).astype(jnp.bfloat16)

    spread = lax.map(place_one, received)
    axis_ids = jnp.arange(grid_side, dtype=jnp.int32)
    live_ids = row_numbers(grid_side)
    cos_w, sin_w = phase_tables(live_ids, axis_ids, grid_side)
    forward_y = jnp.concatenate(
        [jnp.concatenate([cos_w, sin_w], 1), jnp.concatenate([-sin_w, cos_w], 1)], 0
    )
    inverse_y = jnp.concatenate(
        [jnp.concatenate([cos_w.T, -sin_w.T], 1), jnp.concatenate([sin_w.T, cos_w.T], 1)], 0
    )
    cos_x = cos_w.T
    sin_x = sin_w.T
    forward_x = jnp.concatenate([cos_x, sin_x], 0)
    inverse_x = jnp.concatenate([cos_w, sin_w], 0)
    half_y = jnp.dot(
        spread.reshape(-1, 2 * half_side), forward_y, preferred_element_type=jnp.float32
    )
    half_y = half_y.astype(jnp.bfloat16).reshape(planes, depth_count, half_side, 2 * grid_side)
    mixed_x = jnp.einsum("ux,pbxw->pbuw", forward_x, half_y, preferred_element_type=jnp.float32)
    cos_part = mixed_x[:, :, :grid_side]
    sin_part = mixed_x[:, :, grid_side:]
    pot_field = potential_rows[:, None, :, :]
    real_part = (cos_part[..., :grid_side] - sin_part[..., grid_side:]) * pot_field
    imag_part = (cos_part[..., grid_side:] + sin_part[..., :grid_side]) * pot_field
    product = jnp.concatenate([real_part, imag_part], 3).astype(jnp.bfloat16)
    mixed_x = jnp.einsum("ux,pbxw->pbuw", inverse_x, product, preferred_element_type=jnp.float32)
    cos_part = mixed_x[:, :, :half_side]
    sin_part = mixed_x[:, :, half_side:]
    back_x = jnp.concatenate(
        [
            cos_part[..., :grid_side] + sin_part[..., grid_side:],
            cos_part[..., grid_side:] - sin_part[..., :grid_side],
        ],
        3,
    ).astype(jnp.bfloat16)
    back_y = jnp.dot(
        back_x.reshape(-1, 2 * grid_side), inverse_y, preferred_element_type=jnp.float32
    ).astype(jnp.bfloat16)
    back_y = back_y.reshape(planes, depth_count, half_side, 2, half_side)

    def pick_one(grid):
        picked = jnp.einsum("sx,dxcy->dcsy", x_onehot, grid, preferred_element_type=jnp.float32)
        values = jnp.sum(picked * y_onehot[None, None], axis=3)
        values = values.reshape(depth_count, 2, sources, slot_count).transpose(2, 0, 1, 3)
        return values.reshape(-1).astype(jnp.bfloat16)

    return lax.map(pick_one, back_y)


def body(coefficients, potential, stick_map, plane_order):
    band_count = coefficients.shape[0]
    z_span = coefficients.shape[2]
    slot_count = coefficients.shape[3]
    grid_side = potential.shape[1]
    entries = jnp.arange(z_span, dtype=jnp.int32)
    freq_z = (entries - z_span // 2) % grid_side
    half_len = (stick_map[2] - 1) // 2
    keep_mask = jnp.abs(entries[:, None] - z_span // 2) <= half_len[None, :]
    masked = coefficients * keep_mask.astype(jnp.bfloat16)
    cos_z, sin_z = phase_tables(plane_order, freq_z, grid_side)
    forward_z = jnp.stack(
        [jnp.concatenate([cos_z, -sin_z], 1), jnp.concatenate([sin_z, cos_z], 1)], 1
    )
    sticks = jnp.einsum(
        "zck,bks->zbcs",
        forward_z,
        masked.reshape(band_count, 2 * z_span, slot_count),
        preferred_element_type=jnp.float32,
    )
    sticks = sticks.astype(jnp.bfloat16).reshape(grid_side, band_count * 2 * slot_count)
    columns = lax.all_gather(stick_map, "fft", axis=1, tiled=True)
    sources = lax.axis_size("fft")
    x_onehot = one_hot_rows(columns[0], grid_side)
    y_onehot = one_hot_rows(columns[1], grid_side)
    copies = lax.axis_size("sub")
    plane_share = potential.shape[0] // copies
    potential_rows = lax.dynamic_slice_in_dim(
        potential, lax.axis_index("sub") * plane_share, plane_share, 0
    )
    received = lax.all_to_all(sticks, ("fft", "sub"), split_axis=0, concat_axis=1, tiled=True)
    gathered = plane_work(
        received, x_onehot, y_onehot, sources, copies * band_count, grid_side, potential_rows
    )
    returned = lax.all_to_all(gathered, ("fft", "sub"), split_axis=1, concat_axis=0, tiled=True)
    inverse_z = jnp.stack([jnp.stack([cos_z, sin_z], 1), jnp.stack([-sin_z, cos_z], 1)], 1)
    totals = jnp.einsum(
        "rcdk,rbds->bcks",
        inverse_z,
        returned.reshape(grid_side, band_count, 2, slot_count),
        preferred_element_type=jnp.float32,
    )
    return totals * (keep_mask.astype(jnp.float32) * (1.0 / grid_side**3))


def solution(mesh):
    placed = (
        P(("groups", "band", "sub"), None, None, "fft"),
        P(("groups", "fft"), None, None),
        P(None, ("groups", "fft")),
        P("groups"),
    )
    return jax.shard_map(
        body,
        mesh=mesh,
        in_specs=placed,
        out_specs=P(("groups", "band", "sub"), None, None, "fft"),
        check_vma=False,
    )
```

profile of v0, /device:TPU:0, one launch (start us, length us, event | category | flops | bytes accessed | tf_op | source)
XLA Modules:
  0.0 154.8 jit_solution(12331591917178488166)
XLA Ops:
  0.0 1.2 sine_convert_fusion.3
  1.2 1.1 fusion.86
  3.3 0.9 broadcast_multiply_fusion
  4.6 0.8 all_to_all.26
  5.4 6.4 %all-to-all-start = ((bf16[8,24,512]{2,1,0:T(8,128)(2,1)}), bf16[8,24,512]{2,1,0:T(8,128)(2,1)S(1)}, u32[]{:S(2)}, u32[]{:S(2)}) async-start(bf16[8,24,512]{2,1,0:T(8,128)(2,1)} %all_to_all.26), calls=%async_computation | async-start | bytes 393216 | tf_op jit(solution)/shard_map/all_to_all | solution.py:123
  11.8 15.4 %all_gather.3 = s32[3,1024]{1,0:T(4,128)S(1)} all-gather(s32[3,256]{1,0:T(4,128)} %param.10), channel_id=1, replica_groups=mesh['groups'=2,'fft'=4,'band'=2,'sub'=2] {'fft'}, dimensions={1}, use_global_device_ids=true | all-gather | bytes 15360 | tf_op jit(solution)/shard_map/all_gather | solution.py:114
  29.2 1.2 sine_convert_fusion
  30.3 1.1 fusion.87
  31.5 4.9 %constant_dynamic-slice_fusion.1 = f32[24,192,192]{2,1,0:T(8,128)} fusion(f32[48,192,192]{2,1,0:T(8,128)} %param.9, s32[]{:T(128)S(6)} %select_n.131), kind=kLoop, calls=%fused_computation.140 | loop fusion | bytes 7077892 | tf_op jit(solution)/shard_map/dynamic_slice | solution.py:120
  36.4 30.9 %while.22 = (s32[]{:T(128)}, bf16[24,2,96,2,96]{2,1,0,4,3:T(2,128)(2,1)}, bf16[24,4096]{1,0:T(8,128)(2,1)S(1)}, s32[1024]{0:T(1024)S(1)}, s32[1024]{0:T(1024)S(1)}, /*index=5*/s32[]{:T(128)}) while((s32[]{:T(128)}, bf16[24,2,96,2,96]{2,1,0,4,3:T(2,128)(2,1)}, bf16[24,4096]{1,0:T(8,128)(2,1)S(1)}, s32[1024]{0:T(1024)S(1)}, ...), condition=%wide.region_1.2_spmd.clone, body=%wide.region_0.1_spmd.clone.sunk | while | flops 76320768 | bytes 705097 | solution.py:44
  49.9 0.8 copy_dynamic-update-slice_fusion.2
  64.0 0.8 copy_dynamic-update-slice_fusion.2
  67.4 7.0 %reshape.324 = bf16[4608,192]{0,1:T(8,128)(2,1)S(1)} reshape(bf16[24,2,96,2,96]{2,1,0,4,3:T(2,128)(2,1)} %get-tuple-element.59) | data formatting | bytes 3538944 | tf_op jit(solution)/shard_map/reshape | solution.py:59
  74.4 1.5 convolution_convert_fusion.1
  75.9 11.5 %convolution_bitcast_fusion = f32[24,2,384,384]{3,2,1,0:T(8,128)} fusion(bf16[24,2,96,384]{3,2,1,0:T(8,128)(2,1)S(1)} %bitcast.104, bf16[192,96]{0,1:T(8,128)(2,1)S(1)} %get-tuple-element.141, bf16[192,96]{0,1:T(8,128)(2,1)S(1)} %get-tuple-element.140), kind=kOutput, calls=%fused_computation.28 | convolution fusion | flops 1359101952 | bytes 31924224 | tf_op jit(solution)/shard_map/ux,pbxw->pbuw/dot_general | solution.py:62
  87.3 16.3 %fusion.27 = (bf16[24,2,192,192]{3,2,1,0:T(8,128)(2,1)S(1)}, bf16[24,2,192,192]{3,2,1,0:T(8,128)(2,1)}) fusion(f32[24,2,384,384]{3,2,1,0:T(8,128)} %convolution_bitcast_fusion, f32[24,192,192]{2,1,0:T(8,128)S(1)} %bitcast.106), kind=kLoop, calls=%fused_computation.34 | loop fusion | flops 10616832 | bytes 38928384 | tf_op jit(solution)/shard_map/convert.4
  103.6 4.9 %convolution_bitcast_fusion.1 = f32[24,2,192,384]{3,2,1,0:T(8,128)S(1)} fusion(bf16[24,2,192,192]{3,2,1,0:T(8,128)(2,1)} %get-tuple-element.127, bf16[24,2,192,192]{3,2,1,0:T(8,128)(2,1)S(1)} %get-tuple-element.126, bf16[96,192]{1,0:T(8,128)(2,1)S(1)} %get-tuple-element.142, bf16[96,192]{1,0:T(8,128)(2,1)S(1)} %get-tuple-element.143), kind=kOutput, calls=%fused_computation.35 | convolution fusion | flops 1373257728 | bytes 21307392 | tf_op jit(solution)/shard_map/ux,pbxw->pbuw/dot_general | solution.py:69
  108.5 3.1 %fusion.32 = (bf16[24,2,96,192]{3,2,1,0:T(8,128)(2,1)S(1)}, bf16[24,2,96,192]{3,2,1,0:T(8,128)(2,1)S(1)}) fusion(f32[24,2,192,384]{3,2,1,0:T(8,128)S(1)} %convolution_bitcast_fusion.1), kind=kLoop, calls=%fused_computation.44 | loop fusion | flops 3538944 | bytes 17694720 | tf_op jit(solution)/shard_map/convert.3
  111.5 2.8 %convolution_convert_fusion.2 = bf16[4608,192]{0,1:T(8,128)(2,1)} fusion(bf16[4608,192]{1,0:T(8,128)(2,1)S(1)} %bitcast.108, bf16[4608,192]{1,0:T(8,128)(2,1)S(1)} %bitcast.107, bf16[192,96]{0,1:T(8,128)(2,1)S(1)} %get-tuple-element.140, bf16[192,96]{0,1:T(8,128)(2,1)S(1)} %get-tuple-element.141, bf16[192,96]{0,1:T(8,128)(2,1)S(1)} %fusion.85), kind=kOutput, calls=%fused_computation.40 | convolution fusion | flops 688029696 | bytes 5419008 | tf_op jit(solution)/shard_map/dot_general | solution.py:79
  114.3 7.7 %reshape.326 = bf16[24,2,96,2,96]{2,1,0,4,3:T(2,128)(2,1)S(1)} reshape(bf16[4608,192]{0,1:T(8,128)(2,1)} %convolution_convert_fusion.2) | data formatting | bytes 3538944 | tf_op jit(solution)/shard_map/reshape | solution.py:82
  122.0 19.3 %while.23 = (s32[]{:T(128)}, bf16[24,4096]{1,0:T(8,128)(2,1)S(1)}, bf16[24,2,96,2,96]{2,1,0,4,3:T(2,128)(2,1)S(1)}, s32[1024]{0:T(1024)S(1)}, s32[1024]{0:T(1024)S(1)}, /*index=5*/s32[]{:T(128)}, s32[]{:T(128)}) while((s32[]{:T(128)}, bf16[24,4096]{1,0:T(8,128)(2,1)S(1)}, bf16[24,2,96,2,96]{2,1,0,4,3:T(2,128)(2,1)S(1)}, ...), condition=%wide.region_4.5_spmd.clone, body=%wide.region_2.4_spmd.clone.sunk | while | flops 76771328 | bytes 1089621 | solution.py:90
  142.0 3.4 %all-to-all-start.1 = ((bf16[24,8,512]{2,0,1:T(8,128)(2,1)}), bf16[24,8,512]{2,0,1:T(8,128)(2,1)S(1)}, u32[]{:S(2)}, u32[]{:S(2)}) async-start(bf16[24,8,512]{2,0,1:T(8,128)(2,1)} %bitcast.87), calls=%async_computation.1 | async-start | bytes 393216 | tf_op jit(solution)/shard_map/all_to_all | solution.py:127
  145.5 8.1 %all-to-all-done.1 = bf16[24,8,512]{2,0,1:T(8,128)(2,1)S(1)} async-done(((bf16[24,8,512]{2,0,1:T(8,128)(2,1)}), bf16[24,8,512]{2,0,1:T(8,128)(2,1)S(1)}, u32[]{:S(2)}, u32[]{:S(2)}) %all-to-all-start.1) | async-done | bytes 196640 | tf_op jit(solution)/shard_map/all_to_all | solution.py:127
  153.9 0.8 copy.24
  (339 shorter events, 51.0 us)
Async XLA Ops:
  5.4 31.0 %all-to-all-start = ((bf16[8,24,512]{2,1,0:T(8,128)(2,1)}), bf16[8,24,512]{2,1,0:T(8,128)(2,1)S(1)}, u32[]{:S(2)}, u32[]{:S(2)}) async-start(bf16[8,24,512]{2,1,0:T(8,128)(2,1)} %all_to_all.26), calls=%async_computation | async-start | bytes 393216 | tf_op jit(solution)/shard_map/all_to_all | solution.py:123
  74.3 13.0 %slice-start = ((s8[4718592]{0:T(1024)(128)(4,1)}), s8[4194304]{0:T(1024)(128)(4,1)S(1)}, s32[]{:S(2)}) async-start(s8[4718592]{0:T(1024)(128)(4,1)} %bitcast.105), calls=%async_computation.2 | async-start | bytes 8388608
  75.9 11.5 %slice-start.1 = ((s8[4718592]{0:T(1024)(128)(4,1)}), s8[524288]{0:T(1024)(128)(4,1)S(1)}, s32[]{:S(2)}) async-start(s8[4718592]{0:T(1024)(128)(4,1)} %bitcast.105), calls=%async_computation.3 | async-start | bytes 1048576
  142.0 11.6 %all-to-all-start.1 = ((bf16[24,8,512]{2,0,1:T(8,128)(2,1)}), bf16[24,8,512]{2,0,1:T(8,128)(2,1)S(1)}, u32[]{:S(2)}, u32[]{:S(2)}) async-start(bf16[24,8,512]{2,0,1:T(8,128)(2,1)} %bitcast.87), calls=%async_computation.1 | async-start | bytes 393216 | tf_op jit(solution)/shard_map/all_to_all | solution.py:127
where the time goes:
time: 155 us
  local copies, waits for them, and re-layouts  51.1 us (33%)
  matrix products  38.7 us (25%)
  other arithmetic  29.4 us (19%)
  blocking collectives  15.4 us (10%)
  starting transfers between devices  9.75 us (6%)
  waiting for transfers between devices  8.1 us (5%)
  loops' own time  2.11 us (1%)
    another operation x2, other arithmetic  19.3 us
    dynamic_update_slice x24, local copies, waits for them, and re-layouts, plane_work(): spread = lax.map(place_one, received)  18.5 us
    all_gather x1, blocking collectives, body(): columns = lax.all_gather(stick_map, 'fft', axis=1, tiled=True)  15.4 us
    dot_general x1, matrix products, plane_work(): jnp.einsum('ux,pbxw->pbuw', forward_x, half_y, preferred_element_type=jnp...  11.5 us
    dot_general x24, matrix products, pick_one(): jnp.einsum('sx,dxcy->dcsy', x_onehot, grid, preferred_element_type=jnp.fl...  8.95 us
    dot_general x24, matrix products, place_one(): jnp.einsum('sx,dcsy->dxcy', x_onehot, weighted, preferred_element_type=jn...  8.66 us
    all_to_all x1, waiting for transfers between devices, body(): lax.all_to_all(gathered, ('fft', 'sub'), split_axis=1, concat_axis=0, til...  8.1 us
    reshape x1, local copies, waits for them, and re-layouts, plane_work(): back_y = back_y.reshape(planes, depth_count, half_side, 2, half_side)  7.68 us
  transfers between devices with their start and end apart: 2, of which 1 were waited for; matrix products, arithmetic and copies ran while one was open for 6% of the time, Pallas kernels for 0%

commit v1 on v0

v1 whole, which is shorter than its diff:
```python
import functools
import math

import jax
import jax.numpy as jnp
import numpy as np
from jax import lax
from jax.experimental import pallas as pl
from jax.experimental.pallas import tpu as pltpu
from jax.sharding import PartitionSpec as P

F32 = jnp.float32
BF16 = jnp.bfloat16


def angle_tables(left_ids, right_ids, modulus):
    turns = (left_ids[:, None] * right_ids[None, :]) % modulus
    angles = turns * (2.0 * math.pi / modulus)
    return np.cos(angles), np.sin(angles)


def pad_to(array, rows, cols):
    return np.pad(array, ((0, rows - array.shape[0]), (0, cols - array.shape[1])))


def z_constants(grid_side, z_span):
    planes = np.arange(grid_side)
    freq = (np.arange(z_span) - z_span // 2) % grid_side
    cos_z, sin_z = angle_tables(planes, freq, grid_side)
    forward = np.concatenate([cos_z, -sin_z, sin_z, cos_z], 1)
    inverse = np.concatenate([cos_z.T, sin_z.T], 0)
    return jnp.asarray(forward, BF16), jnp.asarray(inverse, BF16)


def axis_constants(grid_side, lane_pad):
    half = grid_side // 2
    quarter = half // 2
    grid_ids = np.arange(grid_side)
    compact = np.arange(half)
    window = np.where(compact < quarter, compact, compact + half)
    cos_w, sin_w = angle_tables(window, grid_ids, grid_side)

    def by_high(top, bottom):
        parts = []
        for high in range(2):
            rows = slice(high * quarter, (high + 1) * quarter)
            parts += [top[rows], bottom[rows]]
        return np.concatenate(parts, 0)

    forward_x = np.concatenate([by_high(cos_w, -sin_w).T, by_high(sin_w, cos_w).T], 0)
    pad = functools.partial(pad_to, rows=lane_pad, cols=grid_side)
    forward_y = np.stack(
        [
            np.concatenate([pad(cos_w), pad(-sin_w)], 0),
            np.concatenate([pad(sin_w), pad(cos_w)], 0),
        ]
    )
    inverse_y = np.stack(
        [
            np.concatenate([pad(cos_w).T, pad(-sin_w).T], 1),
            np.concatenate([pad(sin_w).T, pad(cos_w).T], 1),
        ]
    )
    inverse_x = np.stack([by_high(cos_w, -sin_w), by_high(sin_w, cos_w)])
    return tuple(jnp.asarray(t, BF16) for t in (forward_x, forward_y, inverse_y, inverse_x))


def mm(left, right):
    return jnp.dot(left, right, preferred_element_type=F32)


def mm_t(left, right):
    return lax.dot_general(left, right, (((0,), (0,)), ((), ())), preferred_element_type=F32)


def stick_kernel(coeff, smap, order, fwd, inv, out, table, *, owners, share):
    bands, _, z_span, slots = coeff.shape
    grid_side = order.shape[1]
    chosen = lax.broadcasted_iota(jnp.int32, (grid_side, grid_side), 0) == order[...]
    chosen = chosen.astype(BF16)
    rows = mm_t(chosen, fwd[...]).astype(BF16)
    table[...] = mm(inv[...], chosen).astype(BF16)
    entries = lax.broadcasted_iota(jnp.int32, (z_span, slots), 0)
    half_len = (smap[2:3, :] + 1) // 2 - 1
    keep = jnp.abs(entries - z_span // 2) <= half_len
    for band in range(bands):
        parts = []
        for comp in range(2):
            values = coeff[band, comp].astype(F32)
            parts.append(jnp.where(keep, values, 0.0).astype(BF16))
        masked = jnp.concatenate(parts, 0)
        for comp in range(2):
            sticks = mm(rows[:, comp * 2 * z_span : (comp + 1) * 2 * z_span], masked).astype(BF16)
            col = (band * 2 + comp) * slots
            for owner in range(owners):
                out[owner, 0:share, col : col + slots] = sticks[owner * share : (owner + 1) * share]
    spare = out.shape[1] - share
    places = jnp.concatenate([smap[0:1, :], smap[1:2, :]], 1).astype(F32)
    places = jnp.broadcast_to(places, (spare, 2 * slots)).astype(BF16)
    for owner in range(owners):
        out[owner, share:, 0 : 2 * slots] = places
        if bands > 1:
            out[owner, share:, 2 * slots :] = jnp.zeros((spare, (bands - 1) * 2 * slots), BF16)


def plane_kernel(
    recv, pot, fwd_x, fwd_y, inv_y, inv_x, out, vals, low, high_t, high, acc, *, bands, slots, share, group
):
    sources = recv.shape[0]
    grid_side = pot.shape[1]
    half = grid_side // 2
    quarter = half // 2
    lane_pad = high.shape[0] // 2
    step = pl.program_id(0)

    @pl.when(step == 0)
    def _():
        for src in range(sources):
            cols = slice(src * slots, (src + 1) * slots)
            vals[src] = recv[src, 0:share, :].astype(F32)
            place = recv[src, share:, 0 : 2 * slots].astype(F32)[0:1].astype(jnp.int32)
            compact = jnp.where(place < quarter, place, place - half)
            compact = jnp.clip(compact, 0, half - 1)
            x_id = compact[:, 0:slots]
            y_id = compact[:, slots : 2 * slots]
            x_high = jnp.where(x_id >= quarter, 1, 0)
            x_low = x_id - x_high * quarter
            rows = lax.broadcasted_iota(jnp.int32, (quarter, slots), 0)
            low[:, cols] = jnp.where(rows == x_low, 1.0, 0.0)
            rows = lax.broadcasted_iota(jnp.int32, (2 * lane_pad, slots), 0)
            hot = jnp.where(rows == x_high * lane_pad + y_id, 1.0, 0.0)
            high[:, cols] = hot.astype(BF16)
            high_t[cols, :] = hot.T.astype(BF16)

    base = step * group
    units = [(plane, band) for plane in range(group) for band in range(bands)]
    pairs = [units[i : i + 2] for i in range(0, len(units), 2)]
    low_hot = low[...].astype(BF16)

    def spread(pair):
        stacked = []
        for plane, band in pair:
            for comp in range(2):
                col = (band * 2 + comp) * slots
                pieces = []
                for src in range(sources):
                    row = vals[src, pl.ds(base + plane, 1), col : col + slots]
                    row = jnp.broadcast_to(row, (quarter, slots)).astype(BF16)
                    pieces.append(row * low_hot[:, src * slots : (src + 1) * slots])
                stacked.append(jnp.concatenate(pieces, 1))
        spots = mm(jnp.concatenate(stacked, 0), high_t[...]).astype(BF16)
        lanes = []
        for i in range(len(pair)):
            rows = spots[i * half : (i + 1) * half]
            lanes.append(jnp.concatenate([rows[:, :lane_pad], rows[:, lane_pad:]], 0))
        return jnp.concatenate(lanes, 1)

    def along_x(grid):
        return mm(fwd_x[...], grid).astype(BF16)

    def along_y(grid):
        stacked = []
        for i in range(grid.shape[1] // lane_pad):
            cols = slice(i * lane_pad, (i + 1) * lane_pad)
            stacked.append(jnp.concatenate([grid[:grid_side, cols], grid[grid_side:, cols]], 1))
        stacked = jnp.concatenate(stacked, 0)
        return mm(stacked, fwd_y[0]), mm(stacked, fwd_y[1])

    def times_potential(pair, fields):
        real, imag = [], []
        for i, (plane, _) in enumerate(pair):
            rows = slice(i * grid_side, (i + 1) * grid_side)
            field = pot[plane]
            real.append((fields[0][rows] * field).astype(BF16))
            imag.append((fields[1][rows] * field).astype(BF16))
        return jnp.concatenate(real, 0), jnp.concatenate(imag, 0)

    def back_y(product):
        return (mm(product[0], inv_y[0]) + mm(product[1], inv_y[1])).astype(BF16)

    def back_x(grid):
        count = grid.shape[0] // grid_side
        total = None
        for comp in range(2):
            cols = slice(comp * lane_pad, (comp + 1) * lane_pad)
            rhs = [grid[i * grid_side : (i + 1) * grid_side, cols] for i in range(count)]
            part = mm(inv_x[comp], jnp.concatenate(rhs, 1))
            total = part if total is None else total + part
        return total.astype(BF16)

    def pick(pair, grid):
        stacked = []
        for i in range(len(pair)):
            cols = slice(i * lane_pad, (i + 1) * lane_pad)
            stacked.append(jnp.concatenate([grid[:half, cols], grid[half:, cols]], 1))
        found = mm(jnp.concatenate(stacked, 0), high[...])
        for i, (plane, band) in enumerate(pair):
            for comp in range(2):
                start = i * half + comp * quarter
                line = jnp.sum(found[start : start + quarter] * low[...], axis=0, keepdims=True)
                col = (band * 2 + comp) * slots
                for src in range(sources):
                    acc[src, pl.ds(base + plane, 1), col : col + slots] = line[
                        :, src * slots : (src + 1) * slots
                    ]

    grids = [spread(pair) for pair in pairs]
    grids = [along_x(grid) for grid in grids]
    fields = [along_y(grid) for grid in grids]
    products = [times_potential(pair, field) for pair, field in zip(pairs, fields)]
    grids = [back_y(product) for product in products]
    grids = [back_x(grid) for grid in grids]
    for pair, grid in zip(pairs, grids):
        pick(pair, grid)

    @pl.when(step == pl.num_programs(0) - 1)
    def _():
        for src in range(sources):
            out[src] = acc[src].astype(BF16)


def column_kernel(returned, smap, table, out, *, slots):
    bands, _, z_span, _ = out.shape
    grid_side = returned.shape[0]
    entries = lax.broadcasted_iota(jnp.int32, (z_span, slots), 0)
    half_len = (smap[2:3, :] + 1) // 2 - 1
    keep = jnp.abs(entries - z_span // 2) <= half_len
    scale = jnp.where(keep, 1.0 / grid_side**3, 0.0)
    for band in range(bands):
        real = returned[:, band * 2 * slots : (band * 2 + 1) * slots]
        imag = returned[:, (band * 2 + 1) * slots : (band * 2 + 2) * slots]
        by_real = mm(table[...], real)
        by_imag = mm(table[...], imag)
        out[band, 0] = (by_real[:z_span] + by_imag[z_span:]) * scale
        out[band, 1] = (by_imag[:z_span] - by_real[z_span:]) * scale


def body(coefficients, potential, stick_map, plane_order):
    bands, _, z_span, slots = coefficients.shape
    share, grid_side, _ = potential.shape
    owners = lax.axis_size("fft")
    width = bands * 2 * slots
    lane_pad = -(-(grid_side // 2) // 128) * 128
    rows_sent = (share // 8 + 1) * 8
    order = plane_order.reshape(1, grid_side)
    params = pltpu.CompilerParams(vmem_limit_bytes=48 << 20)

    fwd_z, inv_z = z_constants(grid_side, z_span)
    sent, table = pl.pallas_call(
        functools.partial(stick_kernel, owners=owners, share=share),
        out_shape=(
            jax.ShapeDtypeStruct((owners, rows_sent, width), BF16),
            jax.ShapeDtypeStruct((2 * z_span, grid_side), BF16),
        ),
        compiler_params=params,
        name="sticks",
    )(coefficients, stick_map, order, fwd_z, inv_z)

    received = lax.all_to_all(sent, "fft", split_axis=0, concat_axis=0, tiled=True)

    group = next(g for g in (4, 2, 1) if share % g == 0)
    tables = axis_constants(grid_side, lane_pad)

    def whole(shape):
        return pl.BlockSpec(shape, lambda i: (0,) * len(shape), pipeline_mode=pl.Buffered(1))

    total = owners * slots
    columns = pl.pallas_call(
        functools.partial(plane_kernel, bands=bands, slots=slots, share=share, group=group),
        grid=(share // group,),
        in_specs=[
            whole((owners, rows_sent, width)),
            pl.BlockSpec((group, grid_side, grid_side), lambda i: (i, 0, 0)),
        ]
        + [whole(t.shape) for t in tables],
        out_specs=whole((owners, share, width)),
        out_shape=jax.ShapeDtypeStruct((owners, share, width), BF16),
        scratch_shapes=[
            pltpu.VMEM((owners, share, width), F32),
            pltpu.VMEM((grid_side // 4, total), F32),
            pltpu.VMEM((total, 2 * lane_pad), BF16),
            pltpu.VMEM((2 * lane_pad, total), BF16),
            pltpu.VMEM((owners, share, width), F32),
        ],
        compiler_params=params,
        name="planes",
    )(received, potential, *tables)

    returned = lax.all_to_all(columns, "fft", split_axis=0, concat_axis=0, tiled=True)
    return pl.pallas_call(
        functools.partial(column_kernel, slots=slots),
        out_shape=jax.ShapeDtypeStruct(coefficients.shape, F32),
        compiler_params=params,
        name="columns",
    )(returned.reshape(grid_side, width), stick_map, table)


def solution(mesh):
    placed = (
        P(("groups", "band", "sub"), None, None, "fft"),
        P(("groups", "fft"), None, None),
        P(None, ("groups", "fft")),
        P("groups"),
    )
    return jax.shard_map(
        body,
        mesh=mesh,
        in_specs=placed,
        out_specs=P(("groups", "band", "sub"), None, None, "fft"),
        check_vma=False,
    )
```

time: 155 us -> 55.6 us (0.36)
  local copies, waits for them, and re-layouts: 51.1 us -> 7.83 us
  matrix products: 38.7 us -> 0 us
  other arithmetic: 29.4 us -> 0 us
  Pallas kernels: 0 us -> 23.1 us
  starting transfers between devices: 9.75 us -> 0 us
  blocking collectives: 15.4 us -> 24.3 us
  waiting for transfers between devices: 8.1 us -> 0 us
  loops' own time: 2.11 us -> 0 us
    dot_general x54 -> x0, matrix products: 38.7 us -> none  [the longest x1 11.5 us: plane_work(): jnp.einsum('ux,pbxw->pbuw', forward_x, half_y, preferred_element_type=jnp...]
    all_to_all x0 -> x2, blocking collectives: none -> 24.3 us  [the longest x1 14.3 us: body(): lax.all_to_all(sent, 'fft', split_axis=0, concat_axis=0, tiled=True)]
    dynamic_update_slice x48 -> x0, local copies, waits for them, and re-layouts: 24 us -> none  [the longest x24 18.5 us: plane_work(): spread = lax.map(place_one, received)]
    pallas_call x0 -> x3, Pallas kernels: none -> 23.1 us  [the longest x1 21.7 us: body(): pl.pallas_call(functools.partial(plane_kernel, bands=bands, slots=slots,...]
    another operation x4 -> x0, other arithmetic: 19.4 us -> none
    all_gather x1 -> x0, blocking collectives: 15.4 us -> none  [body(): columns = lax.all_gather(stick_map, 'fft', axis=1, tiled=True)]
    reshape x26 -> x0, local copies, waits for them, and re-layouts: 15.1 us -> none  [the longest x1 7.68 us: plane_work(): back_y = back_y.reshape(planes, depth_count, half_side, 2, half_side)]
    all_to_all x2 -> x0, starting transfers between devices: 9.75 us -> none  [the longest x1 6.35 us: body(): lax.all_to_all(sticks, ('fft', 'sub'), split_axis=0, concat_axis=1, tiled...]
  transfers between devices with their start and end apart: 2 -> 0, of which waited for: 1 -> 0; matrix products, arithmetic and copies ran while one was open for 6% -> 0% of each run, Pallas kernels for 0% -> 0%
where the time goes in v1:
time: 55.6 us; the launch traced here: 55.2 us
  blocking collectives  24.3 us (44%)
  Pallas kernels  23.1 us (42%)
  local copies, waits for them, and re-layouts  7.83 us (14%)
    pallas_call x1, Pallas kernels, body(): pl.pallas_call(functools.partial(plane_kernel, bands=bands, slots=slots,...  21.7 us
    all_to_all x1, blocking collectives, body(): lax.all_to_all(sent, 'fft', split_axis=0, concat_axis=0, tiled=True)  14.3 us
    all_to_all x1, blocking collectives, body(): lax.all_to_all(columns, 'fft', split_axis=0, concat_axis=0, tiled=True)  9.95 us
    unnamed x20, local copies, waits for them, and re-layouts  7.83 us

profile of v1, /device:TPU:0, one launch (start us, length us, event | category | flops | bytes accessed | tf_op | source)
XLA Modules:
  0.0 55.2 jit_solution(16120418380347878030)
XLA Ops:
  0.0 0.0 copy-start.1
  0.0 0.9 %copy-done.1 = bf16[192,512]{1,0:T(8,128)(2,1)S(1)} copy-done((bf16[192,512]{1,0:T(8,128)(2,1)S(1)}, bf16[192,512]{1,0:T(8,128)(2,1)}, u32[]{:S(2)}) %copy-start.1) | copy-done | bytes 196632
  0.9 0.0 copy-start.5
  0.9 0.9 %copy-done.5 = bf16[1,2,128,256]{3,2,1,0:T(8,128)(2,1)S(1)} copy-done((bf16[1,2,128,256]{3,2,1,0:T(8,128)(2,1)S(1)}, bf16[1,2,128,256]{3,2,1,0:T(8,128)(2,1)}, u32[]{:S(2)}) %copy-start.5) | copy-done | bytes 131096
  1.8 0.0 copy-start.6
  1.8 0.9 %copy-done.6 = bf16[256,192]{1,0:T(8,128)(2,1)S(1)} copy-done((bf16[256,192]{1,0:T(8,128)(2,1)S(1)}, bf16[256,192]{1,0:T(8,128)(2,1)}, u32[]{:S(2)}) %copy-start.6) | copy-done | bytes 98328
  2.7 0.0 copy-start.7
  2.7 0.7 %copy-done.7 = s32[3,256]{1,0:T(4,128)S(1)} copy-done((s32[3,256]{1,0:T(4,128)S(1)}, s32[3,256]{1,0:T(4,128)}, u32[]{:S(2)}) %copy-start.7) | copy-done | bytes 3096
  3.4 0.0 copy-start.9
  3.4 0.7 %copy-done.9 = s32[192]{0:T(256)S(1)} copy-done((s32[192]{0:T(256)S(1)}, s32[192]{0:T(256)}, u32[]{:S(2)}) %copy-start.9) | copy-done | bytes 792
  4.1 0.0 copy-start.8
  4.1 0.4 sticks.1
  4.5 14.3 %all_to_all.10.recv = bf16[4,56,512]{2,1,0:T(8,128)(2,1)S(1)} all-to-all(bf16[4,56,512]{2,1,0:T(8,128)(2,1)S(1)} %get-tuple-element.7), channel_id=1, replica_groups=mesh['groups'=2,'fft'=4,'band'=2,'sub'=2] {'fft'}, dimensions={0} | all-to-all | bytes 458752 | tf_op jit(solution)/shard_map/all_to_all | solution.py:259
  18.8 0.0 copy-start
  18.8 0.9 %copy-done = bf16[2,256,192]{2,1,0:T(8,128)(2,1)S(1)} copy-done((bf16[2,256,192]{2,1,0:T(8,128)(2,1)S(1)}, bf16[2,256,192]{2,1,0:T(8,128)(2,1)}, u32[]{:S(2)}) %copy-start) | copy-done | bytes 196632
  19.8 0.9 %copy-done.2 = bf16[2,192,192]{2,1,0:T(8,128)(2,1)S(1)} copy-done((bf16[2,192,192]{2,1,0:T(8,128)(2,1)S(1)}, bf16[2,192,192]{2,1,0:T(8,128)(2,1)}, u32[]{:S(2)}) %copy-start.2) | copy-done | bytes 147480
  20.7 0.0 copy-start.3
  20.7 0.9 %copy-done.3 = bf16[2,192,256]{2,1,0:T(8,128)(2,1)S(1)} copy-done((bf16[2,192,256]{2,1,0:T(8,128)(2,1)S(1)}, bf16[2,192,256]{2,1,0:T(8,128)(2,1)}, u32[]{:S(2)}) %copy-start.3) | copy-done | bytes 196632
  21.6 0.0 copy-start.4
  21.6 0.9 %copy-done.4 = bf16[384,192]{1,0:T(8,128)(2,1)S(1)} copy-done((bf16[384,192]{1,0:T(8,128)(2,1)S(1)}, bf16[384,192]{1,0:T(8,128)(2,1)}, u32[]{:S(2)}) %copy-start.4) | copy-done | bytes 147480
  22.6 21.7 %planes.1 = bf16[4,48,512]{2,1,0:T(8,128)(2,1)S(1)} custom-call(bf16[4,56,512]{2,1,0:T(8,128)(2,1)S(1)} %all_to_all.10.recv, f32[48,192,192]{2,1,0:T(8,128)} %pot.1, bf16[384,192]{1,0:T(8,128)(2,1)S(1)} %copy-done.4, bf16[2,256,192]{2,1,0:T(8,128)(2,1)S(1)} %copy-done, bf16[2,192,256]{2,1,0:T(8,128)(2,1)S(1)} %copy-done.3, bf16[2,192,192]{2,1,0:T(8,128)(2,1)S(1)} %copy-done.2), custom_call_target="tpu_custom_call" | custom-call | tf_op jit(solution)/shard_map/planes/pallas_call | solution.py:268
  44.3 10.0 %all_to_all.11 = bf16[4,48,512]{2,1,0:T(8,128)(2,1)S(1)} all-to-all(bf16[4,48,512]{2,1,0:T(8,128)(2,1)S(1)} %planes.1), channel_id=1, replica_groups=mesh['groups'=2,'fft'=4,'band'=2,'sub'=2] {'fft'}, dimensions={0} | all-to-all | bytes 393216 | tf_op jit(solution)/shard_map/all_to_all | solution.py:289
  54.3 0.0 copy-done.8
  54.3 0.9 %columns.1 = f32[1,2,128,256]{3,2,1,0:T(8,128)} custom-call(bf16[192,512]{1,0:T(8,128)(2,1)S(1)} %bitcast.2, s32[3,256]{1,0:T(4,128)S(1)} %copy-done.8, bf16[256,192]{1,0:T(8,128)(2,1)S(1)} %get-tuple-element.8.table), custom_call_target="tpu_custom_call" | custom-call | tf_op jit(solution)/shard_map/columns/pallas_call | solution.py:290
  (1 shorter events, 0.0 us)
Async XLA Ops:
  0.0 0.9 %copy-start.1 = (bf16[192,512]{1,0:T(8,128)(2,1)S(1)}, bf16[192,512]{1,0:T(8,128)(2,1)}, u32[]{:S(2)}) copy-start(bf16[192,512]{1,0:T(8,128)(2,1)} %constant.12.clone.fwd) | copy-start | bytes 589828
  0.9 0.9 %copy-start.5 = (bf16[1,2,128,256]{3,2,1,0:T(8,128)(2,1)S(1)}, bf16[1,2,128,256]{3,2,1,0:T(8,128)(2,1)}, u32[]{:S(2)}) copy-start(bf16[1,2,128,256]{3,2,1,0:T(8,128)(2,1)} %coeff.1) | copy-start | bytes 393220
  1.8 0.9 %copy-start.6 = (bf16[256,192]{1,0:T(8,128)(2,1)S(1)}, bf16[256,192]{1,0:T(8,128)(2,1)}, u32[]{:S(2)}) copy-start(bf16[256,192]{1,0:T(8,128)(2,1)} %constant.13.clone.inv) | copy-start | bytes 294916
  2.7 0.7 %copy-start.7 = (s32[3,256]{1,0:T(4,128)S(1)}, s32[3,256]{1,0:T(4,128)}, u32[]{:S(2)}) copy-start(s32[3,256]{1,0:T(4,128)} %smap.3) | copy-start | bytes 9220
  3.4 0.7 %copy-start.9 = (s32[192]{0:T(256)S(1)}, s32[192]{0:T(256)}, u32[]{:S(2)}) copy-start(s32[192]{0:T(256)} %param.13) | copy-start | bytes 2308
  4.1 50.2 %copy-start.8 = (s32[3,256]{1,0:T(4,128)S(1)}, s32[3,256]{1,0:T(4,128)}, u32[]{:S(2)}) copy-start(s32[3,256]{1,0:T(4,128)} %smap.3) | copy-start | bytes 9220
  18.8 1.0 %copy-start = (bf16[2,256,192]{2,1,0:T(8,128)(2,1)S(1)}, bf16[2,256,192]{2,1,0:T(8,128)(2,1)}, u32[]{:S(2)}) copy-start(bf16[2,256,192]{2,1,0:T(8,128)(2,1)} %constant.15.clone.fwd_y) | copy-start | bytes 589828
  19.8 0.9 %copy-start.2 = (bf16[2,192,192]{2,1,0:T(8,128)(2,1)S(1)}, bf16[2,192,192]{2,1,0:T(8,128)(2,1)}, u32[]{:S(2)}) copy-start(bf16[2,192,192]{2,1,0:T(8,128)(2,1)} %constant.17.clone.inv_x) | copy-start | bytes 442372
  20.7 0.9 %copy-start.3 = (bf16[2,192,256]{2,1,0:T(8,128)(2,1)S(1)}, bf16[2,192,256]{2,1,0:T(8,128)(2,1)}, u32[]{:S(2)}) copy-start(bf16[2,192,256]{2,1,0:T(8,128)(2,1)} %constant.16.clone.inv_y) | copy-start | bytes 589828
  21.6 0.9 %copy-start.4 = (bf16[384,192]{1,0:T(8,128)(2,1)S(1)}, bf16[384,192]{1,0:T(8,128)(2,1)}, u32[]{:S(2)}) copy-start(bf16[384,192]{1,0:T(8,128)(2,1)} %constant.14.clone.fwd_x) | copy-start | bytes 442372

commit v2 on v1

v2 whole, which is shorter than its diff:
```python
import functools
import math

import jax
import jax.numpy as jnp
import numpy as np
from jax import lax
from jax.experimental import pallas as pl
from jax.experimental.pallas import tpu as pltpu
from jax.sharding import PartitionSpec as P

F32 = jnp.float32
BF16 = jnp.bfloat16


def angle_tables(left_ids, right_ids, modulus):
    turns = (left_ids[:, None] * right_ids[None, :]) % modulus
    angles = turns * (2.0 * math.pi / modulus)
    return np.cos(angles), np.sin(angles)


def pad_to(array, rows, cols):
    return np.pad(array, ((0, rows - array.shape[0]), (0, cols - array.shape[1])))


def z_constants(grid_side, z_span):
    freq = (np.arange(z_span) - z_span // 2) % grid_side
    return jnp.asarray(np.concatenate(angle_tables(np.arange(grid_side), freq, grid_side), 1), BF16)


def axis_constants(grid_side, lane_pad):
    half = grid_side // 2
    quarter = half // 2
    grid_ids = np.arange(grid_side)
    compact = np.arange(half)
    window = np.where(compact < quarter, compact, compact + half)
    cos_w, sin_w = angle_tables(window, grid_ids, grid_side)

    def by_high(top, bottom):
        parts = []
        for high in range(2):
            rows = slice(high * quarter, (high + 1) * quarter)
            parts += [top[rows], bottom[rows]]
        return np.concatenate(parts, 0)

    forward_x = np.concatenate([by_high(cos_w, -sin_w).T, by_high(sin_w, cos_w).T], 0)
    pad = functools.partial(pad_to, rows=lane_pad, cols=grid_side)
    forward_y = np.stack(
        [
            np.concatenate([pad(cos_w), pad(-sin_w)], 0),
            np.concatenate([pad(sin_w), pad(cos_w)], 0),
        ]
    )
    inverse_y = np.stack(
        [
            np.concatenate([pad(cos_w).T, pad(-sin_w).T], 1),
            np.concatenate([pad(sin_w).T, pad(cos_w).T], 1),
        ]
    )
    inverse_x = np.stack([by_high(cos_w, -sin_w), by_high(sin_w, cos_w)])
    return tuple(jnp.asarray(t, BF16) for t in (forward_x, forward_y, inverse_y, inverse_x))


def mm(left, right):
    return jnp.dot(left, right, preferred_element_type=F32)


def mm_t(left, right):
    return lax.dot_general(left, right, (((0,), (0,)), ((), ())), preferred_element_type=F32)


def hops(owners):
    return (0,) + tuple(range(owners - 1, 0, -1))


def partner(index, hop, owners):
    return index ^ hop if owners & (owners - 1) == 0 else (index + hop) % owners


def copies_in(sources, targets, sems):
    started = [
        pltpu.make_async_copy(src, dst, sems.at[i]) for i, (src, dst) in enumerate(zip(sources, targets))
    ]
    for one in started:
        one.start()
    return started


def stick_kernel(me, coeff_h, smap_h, order_h, turn_h, *refs, owners, share):
    outs = refs[:owners]
    table, half_len, coeff, smap, order, turn, sticks, sems = refs[owners:]
    started = copies_in((order_h, turn_h, smap_h, coeff_h), (order, turn, smap, coeff), sems)
    bands, _, z_span, slots = coeff.shape
    grid_side = order.shape[1]
    started[0].wait()
    chosen = lax.broadcasted_iota(jnp.int32, (grid_side, grid_side), 0) == order[...]
    chosen = jnp.where(chosen, 1.0, 0.0).astype(BF16)
    started[1].wait()
    rows = mm_t(chosen, turn[...])
    table[...] = rows.T.astype(BF16)
    rows = rows.astype(BF16)
    cos_rows, sin_rows = rows[:, :z_span], rows[:, z_span:]
    lefts = (
        jnp.concatenate([cos_rows, -sin_rows], 1),
        jnp.concatenate([sin_rows, cos_rows], 1),
    )
    started[2].wait()
    entries = lax.broadcasted_iota(jnp.int32, (z_span, slots), 0)
    half = (smap[2:3, :] + 1) // 2 - 1
    half_len[...] = jnp.broadcast_to(half, half_len.shape)
    keep = jnp.abs(entries - z_span // 2) <= half
    started[3].wait()
    for band in range(bands):
        parts = []
        for comp in range(2):
            values = coeff[band, comp].astype(F32)
            parts.append(jnp.where(keep, values, 0.0).astype(BF16))
        masked = jnp.concatenate(parts, 0)
        for comp in range(2):
            found = mm(lefts[comp], masked).astype(BF16)
            col = (band * 2 + comp) * slots
            for owner in range(owners):
                sticks[owner, :, col : col + slots] = found[owner * share : (owner + 1) * share]
    spare = outs[0].shape[0] - share
    places = jnp.concatenate([smap[0:1, :], smap[1:2, :]], 1).astype(F32)
    places = jnp.broadcast_to(places, (spare, 2 * slots)).astype(BF16)
    for out, hop in zip(outs, hops(owners)):
        out[0:share, :] = sticks[partner(me[0], hop, owners)]
        out[share:, 0 : 2 * slots] = places
        if bands > 1:
            out[share:, 2 * slots :] = jnp.zeros((spare, (bands - 1) * 2 * slots), BF16)


def plane_kernel(*refs, sources, bands, slots, share, group):
    recv = refs[:sources]
    pot_h, *tables_h = refs[sources : sources + 5]
    outs = refs[sources + 5 : 2 * sources + 5]
    pot, fwd_x, fwd_y, inv_y, inv_x, vals, low, high_t, high, acc, table_sems, pot_sems = refs[2 * sources + 5 :]
    grid_side = pot.shape[1]
    half = grid_side // 2
    quarter = half // 2
    lane_pad = high.shape[0] // 2
    started = copies_in(tables_h, (fwd_x, fwd_y, inv_y, inv_x), table_sems)

    def pot_copy(step):
        rows = pl.ds(step * group, group)
        return pltpu.make_async_copy(pot_h.at[rows], pot.at[rows], pot_sems.at[step])

    for step in range(share // group):
        pot_copy(step).start()

    for src in range(sources):
        cols = slice(src * slots, (src + 1) * slots)
        vals[src] = recv[src][0:share, :].astype(F32)
        place = recv[src][share:, 0 : 2 * slots].astype(F32)[0:1].astype(jnp.int32)
        compact = jnp.where(place < quarter, place, place - half)
        compact = jnp.clip(compact, 0, half - 1)
        x_id = compact[:, 0:slots]
        y_id = compact[:, slots : 2 * slots]
        x_high = jnp.where(x_id >= quarter, 1, 0)
        x_low = x_id - x_high * quarter
        rows = lax.broadcasted_iota(jnp.int32, (quarter, slots), 0)
        low[:, cols] = jnp.where(rows == x_low, 1.0, 0.0)
        rows = lax.broadcasted_iota(jnp.int32, (2 * lane_pad, slots), 0)
        hot = jnp.where(rows == x_high * lane_pad + y_id, 1.0, 0.0)
        high[:, cols] = hot.astype(BF16)
        high_t[cols, :] = hot.T.astype(BF16)

    for one in started:
        one.wait()

    def one_group(step):
        base = step * group
        units = [(plane, band) for plane in range(group) for band in range(bands)]
        pairs = [units[i : i + 2] for i in range(0, len(units), 2)]
        low_hot = low[...].astype(BF16)

        def spread(pair):
            stacked = []
            for plane, band in pair:
                for comp in range(2):
                    col = (band * 2 + comp) * slots
                    pieces = []
                    for src in range(sources):
                        row = vals[src, pl.ds(base + plane, 1), col : col + slots]
                        row = jnp.broadcast_to(row, (quarter, slots)).astype(BF16)
                        pieces.append(row * low_hot[:, src * slots : (src + 1) * slots])
                    stacked.append(jnp.concatenate(pieces, 1))
            spots = mm(jnp.concatenate(stacked, 0), high_t[...]).astype(BF16)
            lanes = []
            for i in range(len(pair)):
                rows = spots[i * half : (i + 1) * half]
                lanes.append(jnp.concatenate([rows[:, :lane_pad], rows[:, lane_pad:]], 0))
            return jnp.concatenate(lanes, 1)

        def along_x(grid):
            return mm(fwd_x[...], grid).astype(BF16)

        def along_y(grid):
            stacked = []
            for i in range(grid.shape[1] // lane_pad):
                cols = slice(i * lane_pad, (i + 1) * lane_pad)
                stacked.append(jnp.concatenate([grid[:grid_side, cols], grid[grid_side:, cols]], 1))
            stacked = jnp.concatenate(stacked, 0)
            return mm(stacked, fwd_y[0]), mm(stacked, fwd_y[1])

        def times_potential(pair, fields):
            real, imag = [], []
            for i, (plane, _) in enumerate(pair):
                rows = slice(i * grid_side, (i + 1) * grid_side)
                field = pot[base + plane]
                real.append((fields[0][rows] * field).astype(BF16))
                imag.append((fields[1][rows] * field).astype(BF16))
            return jnp.concatenate(real, 0), jnp.concatenate(imag, 0)

        def back_y(product):
            return (mm(product[0], inv_y[0]) + mm(product[1], inv_y[1])).astype(BF16)

        def back_x(grid):
            count = grid.shape[0] // grid_side
            total = None
            for comp in range(2):
                cols = slice(comp * lane_pad, (comp + 1) * lane_pad)
                rhs = [grid[i * grid_side : (i + 1) * grid_side, cols] for i in range(count)]
                part = mm(inv_x[comp], jnp.concatenate(rhs, 1))
                total = part if total is None else total + part
            return total.astype(BF16)

        def pick(pair, grid):
            stacked = []
            for i in range(len(pair)):
                cols = slice(i * lane_pad, (i + 1) * lane_pad)
                stacked.append(jnp.concatenate([grid[:half, cols], grid[half:, cols]], 1))
            found = mm(jnp.concatenate(stacked, 0), high[...])
            for i, (plane, band) in enumerate(pair):
                for comp in range(2):
                    start = i * half + comp * quarter
                    line = jnp.sum(found[start : start + quarter] * low[...], axis=0, keepdims=True)
                    col = (band * 2 + comp) * slots
                    for src in range(sources):
                        acc[src, pl.ds(base + plane, 1), col : col + slots] = line[
                            :, src * slots : (src + 1) * slots
                        ]

        grids = [spread(pair) for pair in pairs]
        grids = [along_x(grid) for grid in grids]
        fields = [along_y(grid) for grid in grids]
        products = [times_potential(pair, field) for pair, field in zip(pairs, fields)]
        grids = [back_y(product) for product in products]
        grids = [back_x(grid) for grid in grids]
        for pair, grid in zip(pairs, grids):
            pick(pair, grid)

    @pl.loop(0, share // group)
    def _(step):
        pot_copy(step).wait()
        one_group(step)

    for src in range(sources):
        outs[src][...] = acc[src].astype(BF16)


def column_kernel(me, half_len, table, *refs, owners, slots):
    returned, (out, grid) = refs[:owners], refs[owners:]
    bands, _, z_span, _ = out.shape
    for part, hop in zip(returned, hops(owners)):
        grid[partner(me[0], hop, owners)] = part[...]
    entries = lax.broadcasted_iota(jnp.int32, (z_span, slots), 0)
    keep = jnp.abs(entries - z_span // 2) <= half_len[0:1, :]
    grid_side = table.shape[1]
    scale = jnp.where(keep, 1.0 / grid_side**3, 0.0)
    for band in range(bands):
        lines = []
        for comp in range(2):
            col = (band * 2 + comp) * slots
            lines.append(
                jnp.concatenate([grid[owner, :, col : col + slots] for owner in range(owners)], 0)
            )
        by_real = mm(table[...], lines[0])
        by_imag = mm(table[...], lines[1])
        out[band, 0] = (by_real[:z_span] + by_imag[z_span:]) * scale
        out[band, 1] = (by_imag[:z_span] - by_real[z_span:]) * scale


def exchange(parts, owners, back):
    result = [parts[0]]
    for part, hop in zip(parts[1:], hops(owners)[1:]):
        pairs = [(i, partner(i, hop, owners)) for i in range(owners)]
        if back:
            pairs = [(there, here) for here, there in pairs]
        with jax.named_scope(("back" if back else "send") + str(hop)):
            result.append(lax.ppermute(part, "fft", pairs))
    return result


def body(coefficients, potential, stick_map, plane_order):
    bands, _, z_span, slots = coefficients.shape
    share, grid_side, _ = potential.shape
    owners = lax.axis_size("fft")
    width = bands * 2 * slots
    lane_pad = -(-(grid_side // 2) // 128) * 128
    rows_sent = (share // 8 + 1) * 8
    params = pltpu.CompilerParams(vmem_limit_bytes=48 << 20)
    me = lax.axis_index("fft").astype(jnp.int32).reshape(1)
    in_smem = pl.BlockSpec(memory_space=pltpu.SMEM)
    in_hbm = pl.BlockSpec(memory_space=pltpu.HBM)
    in_vmem = pl.BlockSpec(memory_space=pltpu.VMEM)

    def stay(*arrays):
        return tuple(pltpu.with_memory_space_constraint(one, pltpu.HBM) for one in arrays)

    *sent, table, half_len = pl.pallas_call(
        functools.partial(stick_kernel, owners=owners, share=share),
        in_specs=[in_smem] + [in_hbm] * 4,
        out_shape=[jax.ShapeDtypeStruct((rows_sent, width), BF16)] * owners
        + [
            jax.ShapeDtypeStruct((2 * z_span, grid_side), BF16),
            jax.ShapeDtypeStruct((8, slots), jnp.int32),
        ],
        scratch_shapes=[
            pltpu.VMEM(coefficients.shape, BF16),
            pltpu.VMEM(stick_map.shape, jnp.int32),
            pltpu.VMEM((1, grid_side), jnp.int32),
            pltpu.VMEM((grid_side, 2 * z_span), BF16),
            pltpu.VMEM((owners, share, width), BF16),
            pltpu.SemaphoreType.DMA((4,)),
        ],
        compiler_params=params,
        name="sticks",
    )(
        me,
        *stay(
            coefficients, stick_map, plane_order.reshape(1, grid_side), z_constants(grid_side, z_span)
        ),
    )

    received = exchange(sent, owners, False)

    group = next(g for g in (8, 4, 2, 1) if share % g == 0)
    tables = axis_constants(grid_side, lane_pad)
    total = owners * slots
    columns = pl.pallas_call(
        functools.partial(
            plane_kernel, sources=owners, bands=bands, slots=slots, share=share, group=group
        ),
        in_specs=[in_vmem] * owners + [in_hbm] * 5,
        out_shape=[jax.ShapeDtypeStruct((share, width), BF16)] * owners,
        scratch_shapes=[pltpu.VMEM(potential.shape, F32)]
        + [pltpu.VMEM(t.shape, BF16) for t in tables]
        + [
            pltpu.VMEM((owners, share, width), F32),
            pltpu.VMEM((grid_side // 4, total), F32),
            pltpu.VMEM((total, 2 * lane_pad), BF16),
            pltpu.VMEM((2 * lane_pad, total), BF16),
            pltpu.VMEM((owners, share, width), F32),
            pltpu.SemaphoreType.DMA((4,)),
            pltpu.SemaphoreType.DMA((share // group,)),
        ],
        compiler_params=params,
        name="planes",
    )(*received, *stay(potential, *tables))

    returned = exchange(columns, owners, True)
    return pl.pallas_call(
        functools.partial(column_kernel, owners=owners, slots=slots),
        in_specs=[in_smem] + [in_vmem] * (owners + 2),
        out_shape=jax.ShapeDtypeStruct(coefficients.shape, F32),
        scratch_shapes=[pltpu.VMEM((owners, share, width), BF16)],
        compiler_params=params,
        name="columns",
    )(me, half_len, table, *returned)


def solution(mesh):
    placed = (
        P(("groups", "band", "sub"), None, None, "fft"),
        P(("groups", "fft"), None, None),
        P(None, ("groups", "fft")),
        P("groups"),
    )
    return jax.shard_map(
        body,
        mesh=mesh,
        in_specs=placed,
        out_specs=P(("groups", "band", "sub"), None, None, "fft"),
        check_vma=False,
    )
```

time: 55.6 us -> 38.1 us (0.69)
  blocking collectives: 24.3 us -> 0 us
  starting transfers between devices: 0 us -> 10.2 us
  local copies, waits for them, and re-layouts: 7.83 us -> 0 us
  waiting for transfers between devices: 0 us -> 7.68 us
  Pallas kernels: 23.1 us -> 20 us
    all_to_all x2 -> x0, blocking collectives: 24.3 us -> none  [the longest x1 14.3 us: body(): lax.all_to_all(sent, 'fft', split_axis=0, concat_axis=0, tiled=True)]
    ppermute x0 -> x6, starting transfers between devices: none -> 10.2 us  [exchange(): result.append(lax.ppermute(part, 'fft', pairs))]
    unnamed x20 -> x0, local copies, waits for them, and re-layouts: 7.83 us -> none
    ppermute x0 -> x6, waiting for transfers between devices: none -> 7.68 us  [exchange(): result.append(lax.ppermute(part, 'fft', pairs))]
    pallas_call x2, Pallas kernels: 22.6 us -> 18.5 us  [the longest x1 17.5 us: body(): pl.pallas_call(functools.partial(plane_kernel, sources=owners, bands=band...]
    pallas_call x1, Pallas kernels: 0.41 us -> 1.51 us  [body(): pl.pallas_call(functools.partial(stick_kernel, owners=owners, share=share...]
  transfers between devices with their start and end apart: 0 -> 6, of which waited for: 0 -> 4; matrix products, arithmetic and copies ran while one was open for 0% -> 0% of each run, Pallas kernels for 0% -> 0%
where the time goes in v2:
time: 38.1 us; the launch traced here: 37.9 us
  Pallas kernels  20 us (52%)
  starting transfers between devices  10.2 us (27%)
  waiting for transfers between devices  7.68 us (20%)
    pallas_call x1, Pallas kernels, body(): pl.pallas_call(functools.partial(plane_kernel, sources=owners, bands=band...  17.5 us
    ppermute x6, starting transfers between devices, exchange(): result.append(lax.ppermute(part, 'fft', pairs))  10.2 us
    ppermute x6, waiting for transfers between devices, exchange(): result.append(lax.ppermute(part, 'fft', pairs))  7.68 us
    pallas_call x1, Pallas kernels, body(): pl.pallas_call(functools.partial(stick_kernel, owners=owners, share=share...  1.51 us
    pallas_call x1, Pallas kernels, body(): pl.pallas_call(functools.partial(column_kernel, owners=owners, slots=slot...  0.94 us
  transfers between devices with their start and end apart: 6, of which 4 were waited for; matrix products, arithmetic and copies ran while one was open for 0% of the time, Pallas kernels for 0%

profile of v2, /device:TPU:0, one launch (start us, length us, event | category | flops | bytes accessed | tf_op | source)
XLA Modules:
  0.0 37.9 jit_solution(11978807214982932654)
XLA Ops:
  0.0 1.5 %sticks.1 = (bf16[56,512]{1,0:T(8,128)(2,1)S(1)}, bf16[56,512]{1,0:T(8,128)(2,1)S(1)}, bf16[56,512]{1,0:T(8,128)(2,1)S(1)}, bf16[56,512]{1,0:T(8,128)(2,1)S(1)},...) custom-call(s32[1]{0:T(128)} %bitcast.me, bf16[1,2,128,256]{3,2,1,0:T(8,128)(2,1)} %coeff_h.1, s32[3,256]{1,0:T(4,128)} %smap_h.1, ...), custom_call_target="tpu_custom_call" | custom-call | tf_op jit(solution)/shard_map/sticks/pallas_call | solution.py:312
  1.5 5.1 %collective-permute-start = (bf16[56,512]{1,0:T(8,128)(2,1)S(1)}, bf16[56,512]{1,0:T(8,128)(2,1)S(1)}, u32[]{:S(2)}, u32[]{:S(2)}) collective-permute-start(bf16[56,512]{1,0:T(8,128)(2,1)S(1)} %get-tuple-element.18), channel_id=1, source_target_pairs={{0,12},{4,8},{8,4},{12,0},{1,13},{5,9},{9,5},{13,1},{2,14},{6,10},... | collective-permute-start | bytes 172040 | tf_op jit(solution)/shard_map/send3/ppermute | solution.py:292
  6.7 0.0 collective-permute-start.1
  6.7 0.6 %collective-permute-start.2 = (bf16[56,512]{1,0:T(8,128)(2,1)S(1)}, bf16[56,512]{1,0:T(8,128)(2,1)S(1)}, u32[]{:S(2)}, u32[]{:S(2)}) collective-permute-start(bf16[56,512]{1,0:T(8,128)(2,1)S(1)} %get-tuple-element.20), channel_id=1, source_target_pairs={{0,4},{4,0},{8,12},{12,8},{1,5},{5,1},{9,13},{13,9},{2,6},{6,2},{1... | collective-permute-start | bytes 172040 | tf_op jit(solution)/shard_map/send1/ppermute | solution.py:292
  7.3 1.7 %collective-permute-done.refs_1_ = bf16[56,512]{1,0:T(8,128)(2,1)S(1)} collective-permute-done((bf16[56,512]{1,0:T(8,128)(2,1)S(1)}, bf16[56,512]{1,0:T(8,128)(2,1)S(1)}, u32[]{:S(2)}, u32[]{:S(2)}) %collective-permute-start) | collective-permute-done | bytes 57376 | tf_op jit(solution)/shard_map/send3/ppermute | solution.py:292
  9.0 2.8 %collective-permute-done.1.refs_2_ = bf16[56,512]{1,0:T(8,128)(2,1)S(1)} collective-permute-done((bf16[56,512]{1,0:T(8,128)(2,1)S(1)}, bf16[56,512]{1,0:T(8,128)(2,1)S(1)}, u32[]{:S(2)}, u32[]{:S(2)}) %collective-permute-start.1) | collective-permute-done | bytes 57376 | tf_op jit(solution)/shard_map/send2/ppermute | solution.py:292
  11.7 0.0 collective-permute-done.2.refs_3_
  11.7 17.5 %planes.1 = (bf16[48,512]{1,0:T(8,128)(2,1)S(1)}, bf16[48,512]{1,0:T(8,128)(2,1)S(1)}, bf16[48,512]{1,0:T(8,128)(2,1)S(1)}, bf16[48,512]{1,0:T(8,128)(2,1)S(1)}) custom-call(bf16[56,512]{1,0:T(8,128)(2,1)S(1)} %get-tuple-element.17.refs_0_, bf16[56,512]{1,0:T(8,128)(2,1)S(1)} %collective-permute-done.refs_1_, ...), custom_call_target="tpu_custom_call" | custom-call | tf_op jit(solution)/shard_map/planes/pallas_call | solution.py:342
  29.3 2.7 %collective-permute-start.3 = (bf16[48,512]{1,0:T(8,128)(2,1)S(1)}, bf16[48,512]{1,0:T(8,128)(2,1)S(1)}, u32[]{:S(2)}, u32[]{:S(2)}) collective-permute-start(bf16[48,512]{1,0:T(8,128)(2,1)S(1)} %get-tuple-element.22), channel_id=1, source_target_pairs={{12,0},{8,4},{4,8},{0,12},{13,1},{9,5},{5,9},{1,13},{14,2},{10,6},... | collective-permute-start | bytes 147464 | tf_op jit(solution)/shard_map/back3/ppermute | solution.py:292
  32.0 0.0 collective-permute-start.4
  32.0 1.7 %collective-permute-start.5 = (bf16[48,512]{1,0:T(8,128)(2,1)S(1)}, bf16[48,512]{1,0:T(8,128)(2,1)S(1)}, u32[]{:S(2)}, u32[]{:S(2)}) collective-permute-start(bf16[48,512]{1,0:T(8,128)(2,1)S(1)} %get-tuple-element.24), channel_id=1, source_target_pairs={{4,0},{0,4},{12,8},{8,12},{5,1},{1,5},{13,9},{9,13},{6,2},{2,6},{1... | collective-permute-start | bytes 147464 | tf_op jit(solution)/shard_map/back1/ppermute | solution.py:292
  33.7 1.7 %collective-permute-done.3.refs_1_ = bf16[48,512]{1,0:T(8,128)(2,1)S(1)} collective-permute-done((bf16[48,512]{1,0:T(8,128)(2,1)S(1)}, bf16[48,512]{1,0:T(8,128)(2,1)S(1)}, u32[]{:S(2)}, u32[]{:S(2)}) %collective-permute-start.3) | collective-permute-done | bytes 49184 | tf_op jit(solution)/shard_map/back3/ppermute | solution.py:292
  35.4 1.6 %collective-permute-done.4.refs_2_ = bf16[48,512]{1,0:T(8,128)(2,1)S(1)} collective-permute-done((bf16[48,512]{1,0:T(8,128)(2,1)S(1)}, bf16[48,512]{1,0:T(8,128)(2,1)S(1)}, u32[]{:S(2)}, u32[]{:S(2)}) %collective-permute-start.4) | collective-permute-done | bytes 49184 | tf_op jit(solution)/shard_map/back2/ppermute | solution.py:292
  37.0 0.0 collective-permute-done.5.refs_3_
  37.0 0.9 %columns.1 = f32[1,2,128,256]{3,2,1,0:T(8,128)} custom-call(s32[1]{0:T(128)} %bitcast.me, s32[8,256]{1,0:T(8,128)S(1)} %get-tuple-element.15.half_len, bf16[256,192]{1,0:T(8,128)(2,1)S(1)} %get-tuple-element.16.table, bf16[48,512]{1,0:T(8,128)(2,1)S(1)} %get-tuple-element.21.refs_0_, bf16[48,512]{1,0:T(8,128)(2,1)S(1)} %collective-permute-done.3.refs_1_, ...), custom_call_target="tpu_custom_call" | custom-call | tf_op jit(solution)/shard_map/columns/pallas_call | solution.py:364
Async XLA Ops:
  1.5 7.5 %collective-permute-start = (bf16[56,512]{1,0:T(8,128)(2,1)S(1)}, bf16[56,512]{1,0:T(8,128)(2,1)S(1)}, u32[]{:S(2)}, u32[]{:S(2)}) collective-permute-start(bf16[56,512]{1,0:T(8,128)(2,1)S(1)} %get-tuple-element.18), channel_id=1, source_target_pairs={{0,12},{4,8},{8,4},{12,0},{1,13},{5,9},{9,5},{13,1},{2,14},{6,10},... | collective-permute-start | bytes 172040 | tf_op jit(solution)/shard_map/send3/ppermute | solution.py:292
  6.7 5.1 %collective-permute-start.1 = (bf16[56,512]{1,0:T(8,128)(2,1)S(1)}, bf16[56,512]{1,0:T(8,128)(2,1)S(1)}, u32[]{:S(2)}, u32[]{:S(2)}) collective-permute-start(bf16[56,512]{1,0:T(8,128)(2,1)S(1)} %get-tuple-element.19), channel_id=1, source_target_pairs={{0,8},{4,12},{8,0},{12,4},{1,9},{5,13},{9,1},{13,5},{2,10},{6,14},... | collective-permute-start | bytes 172040 | tf_op jit(solution)/shard_map/send2/ppermute | solution.py:292
  6.7 5.1 %collective-permute-start.2 = (bf16[56,512]{1,0:T(8,128)(2,1)S(1)}, bf16[56,512]{1,0:T(8,128)(2,1)S(1)}, u32[]{:S(2)}, u32[]{:S(2)}) collective-permute-start(bf16[56,512]{1,0:T(8,128)(2,1)S(1)} %get-tuple-element.20), channel_id=1, source_target_pairs={{0,4},{4,0},{8,12},{12,8},{1,5},{5,1},{9,13},{13,9},{2,6},{6,2},{1... | collective-permute-start | bytes 172040 | tf_op jit(solution)/shard_map/send1/ppermute | solution.py:292
  29.3 6.1 %collective-permute-start.3 = (bf16[48,512]{1,0:T(8,128)(2,1)S(1)}, bf16[48,512]{1,0:T(8,128)(2,1)S(1)}, u32[]{:S(2)}, u32[]{:S(2)}) collective-permute-start(bf16[48,512]{1,0:T(8,128)(2,1)S(1)} %get-tuple-element.22), channel_id=1, source_target_pairs={{12,0},{8,4},{4,8},{0,12},{13,1},{9,5},{5,9},{1,13},{14,2},{10,6},... | collective-permute-start | bytes 147464 | tf_op jit(solution)/shard_map/back3/ppermute | solution.py:292
  32.0 5.0 %collective-permute-start.4 = (bf16[48,512]{1,0:T(8,128)(2,1)S(1)}, bf16[48,512]{1,0:T(8,128)(2,1)S(1)}, u32[]{:S(2)}, u32[]{:S(2)}) collective-permute-start(bf16[48,512]{1,0:T(8,128)(2,1)S(1)} %get-tuple-element.23), channel_id=1, source_target_pairs={{8,0},{12,4},{0,8},{4,12},{9,1},{13,5},{1,9},{5,13},{10,2},{14,6},... | collective-permute-start | bytes 147464 | tf_op jit(solution)/shard_map/back2/ppermute | solution.py:292
  32.0 5.0 %collective-permute-start.5 = (bf16[48,512]{1,0:T(8,128)(2,1)S(1)}, bf16[48,512]{1,0:T(8,128)(2,1)S(1)}, u32[]{:S(2)}, u32[]{:S(2)}) collective-permute-start(bf16[48,512]{1,0:T(8,128)(2,1)S(1)} %get-tuple-element.24), channel_id=1, source_target_pairs={{4,0},{0,4},{12,8},{8,12},{5,1},{1,5},{13,9},{9,13},{6,2},{2,6},{1... | collective-permute-start | bytes 147464 | tf_op jit(solution)/shard_map/back1/ppermute | solution.py:292

commit v3 on v2

--- a/solution.py
+++ b/solution.py
@@ -11,6 +11,15 @@
 
 F32 = jnp.float32
 BF16 = jnp.bfloat16
+PARAMS = pltpu.CompilerParams(vmem_limit_bytes=28 << 20)
+IN_SMEM = pl.BlockSpec(memory_space=pltpu.SMEM)
+IN_HBM = pl.BlockSpec(memory_space=pltpu.HBM)
+IN_VMEM = pl.BlockSpec(memory_space=pltpu.VMEM)
+GROUPS = (8, 4, 2, 1)
+
+
+def stay(*arrays):
+    return tuple(pltpu.with_memory_space_constraint(one, pltpu.HBM) for one in arrays)
 
 
 def angle_tables(left_ids, right_ids, modulus):
@@ -122,7 +131,8 @@
             for owner in range(owners):
                 sticks[owner, :, col : col + slots] = found[owner * share : (owner + 1) * share]
     spare = outs[0].shape[0] - share
-    places = jnp.concatenate([smap[0:1, :], smap[1:2, :]], 1).astype(F32)
+    x_id = jnp.where(half >= 0, smap[0:1, :], grid_side)
+    places = jnp.concatenate([x_id, smap[1:2, :]], 1).astype(F32)
     places = jnp.broadcast_to(places, (spare, 2 * slots)).astype(BF16)
     for out, hop in zip(outs, hops(owners)):
         out[0:share, :] = sticks[partner(me[0], hop, owners)]
@@ -133,41 +143,53 @@
 
 def plane_kernel(*refs, sources, bands, slots, share, group):
     recv = refs[:sources]
-    pot_h, *tables_h = refs[sources : sources + 5]
+    pot, fwd_x, fwd_y, inv_y, inv_x = refs[sources : sources + 5]
     outs = refs[sources + 5 : 2 * sources + 5]
-    pot, fwd_x, fwd_y, inv_y, inv_x, vals, low, high_t, high, acc, table_sems, pot_sems = refs[2 * sources + 5 :]
+    vals, select, low, high_t, high, acc = refs[2 * sources + 5 :]
     grid_side = pot.shape[1]
     half = grid_side // 2
     quarter = half // 2
     lane_pad = high.shape[0] // 2
-    started = copies_in(tables_h, (fwd_x, fwd_y, inv_y, inv_x), table_sems)
-
-    def pot_copy(step):
-        rows = pl.ds(step * group, group)
-        return pltpu.make_async_copy(pot_h.at[rows], pot.at[rows], pot_sems.at[step])
-
-    for step in range(share // group):
-        pot_copy(step).start()
-
+
+    live_count = low.shape[1]
+    upper = lax.broadcasted_iota(jnp.int32, (slots, slots), 0)
+    upper = upper < lax.broadcasted_iota(jnp.int32, (slots, slots), 1)
+    upper = jnp.where(upper, 1.0, 0.0).astype(BF16)
+    before = jnp.zeros((1, 1), F32)
+    gathered = None
     for src in range(sources):
         cols = slice(src * slots, (src + 1) * slots)
-        vals[src] = recv[src][0:share, :].astype(F32)
-        place = recv[src][share:, 0 : 2 * slots].astype(F32)[0:1].astype(jnp.int32)
-        compact = jnp.where(place < quarter, place, place - half)
-        compact = jnp.clip(compact, 0, half - 1)
-        x_id = compact[:, 0:slots]
-        y_id = compact[:, slots : 2 * slots]
-        x_high = jnp.where(x_id >= quarter, 1, 0)
-        x_low = x_id - x_high * quarter
-        rows = lax.broadcasted_iota(jnp.int32, (quarter, slots), 0)
-        low[:, cols] = jnp.where(rows == x_low, 1.0, 0.0)
-        rows = lax.broadcasted_iota(jnp.int32, (2 * lane_pad, slots), 0)
-        hot = jnp.where(rows == x_high * lane_pad + y_id, 1.0, 0.0)
-        high[:, cols] = hot.astype(BF16)
-        high_t[cols, :] = hot.T.astype(BF16)
-
-    for one in started:
-        one.wait()
+        places = recv[src][share:, 0:slots].astype(F32)
+        live = jnp.where(places < grid_side, 1.0, 0.0)
+        rank = mm(live.astype(BF16), upper)[0:1] + before
+        live = live[0:1]
+        before = before + jnp.sum(live, axis=1, keepdims=True)
+        rank = jnp.where(live > 0.0, rank, -1.0).astype(jnp.int32)
+        numbers = lax.broadcasted_iota(jnp.int32, (live_count, slots), 0)
+        chosen = jnp.where(numbers == rank, 1.0, 0.0).astype(BF16)
+        select[:, cols] = chosen
+        pieces = [recv[src][:, i * slots : (i + 1) * slots] for i in range(2 * bands)]
+        part = lax.dot_general(
+            jnp.concatenate(pieces, 0), chosen, (((1,), (1,)), ((), ())), preferred_element_type=F32
+        )
+        gathered = part if gathered is None else gathered + part
+    vals[...] = gathered
+    rows_sent = recv[0].shape[0]
+
+    def compacted(row):
+        ids = row.astype(jnp.int32)
+        return jnp.clip(jnp.where(ids < quarter, ids, ids - half), 0, half - 1)
+
+    x_id = compacted(gathered[share : share + 1])
+    y_id = compacted(gathered[rows_sent + share : rows_sent + share + 1])
+    x_high = jnp.where(x_id >= quarter, 1, 0)
+    x_low = x_id - x_high * quarter
+    rows = lax.broadcasted_iota(jnp.int32, (quarter, live_count), 0)
+    low[...] = jnp.where(rows == x_low, 1.0, 0.0)
+    rows = lax.broadcasted_iota(jnp.int32, (2 * lane_pad, live_count), 0)
+    hot = jnp.where(rows == x_high * lane_pad + y_id, 1.0, 0.0)
+    high[...] = hot.astype(BF16)
+    high_t[...] = hot.T.astype(BF16)
 
     def one_group(step):
         base = step * group
@@ -179,13 +201,8 @@
             stacked = []
             for plane, band in pair:
                 for comp in range(2):
-                    col = (band * 2 + comp) * slots
-                    pieces = []
-                    for src in range(sources):
-                        row = vals[src, pl.ds(base + plane, 1), col : col + slots]
-                        row = jnp.broadcast_to(row, (quarter, slots)).astype(BF16)
-                        pieces.append(row * low_hot[:, src * slots : (src + 1) * slots])
-                    stacked.append(jnp.concatenate(pieces, 1))
+                    row = vals[pl.ds((band * 2 + comp) * rows_sent + base + plane, 1), :]
+                    stacked.append(jnp.broadcast_to(row, low_hot.shape).astype(BF16) * low_hot)
             spots = mm(jnp.concatenate(stacked, 0), high_t[...]).astype(BF16)
             lanes = []
             for i in range(len(pair)):
@@ -236,11 +253,7 @@
                 for comp in range(2):
                     start = i * half + comp * quarter
                     line = jnp.sum(found[start : start + quarter] * low[...], axis=0, keepdims=True)
-                    col = (band * 2 + comp) * slots
-                    for src in range(sources):
-                        acc[src, pl.ds(base + plane, 1), col : col + slots] = line[
-                            :, src * slots : (src + 1) * slots
-                        ]
+                    acc[pl.ds((band * 2 + comp) * share + base + plane, 1), :] = line
 
         grids = [spread(pair) for pair in pairs]
         grids = [along_x(grid) for grid in grids]
@@ -253,11 +266,14 @@
 
     @pl.loop(0, share // group)
     def _(step):
-        pot_copy(step).wait()
         one_group(step)
 
+    spread_out = mm(acc[...].astype(BF16), select[...]).astype(BF16)
     for src in range(sources):
-        outs[src][...] = acc[src].astype(BF16)
+        for i in range(2 * bands):
+            outs[src][:, i * slots : (i + 1) * slots] = spread_out[
+                i * share : (i + 1) * share, src * slots : (src + 1) * slots
+            ]
 
 
 def column_kernel(me, half_len, table, *refs, owners, slots):
@@ -293,25 +309,66 @@
     return result
 
 
+def preload_kernel(*refs):
+    count = len(refs) // 2
+    for one in copies_in(refs[:count], refs[count : 2 * count], refs[2 * count]):
+        one.wait()
+
+
+def preload(arrays):
+    return pl.pallas_call(
+        preload_kernel,
+        in_specs=[IN_HBM] * len(arrays),
+        out_specs=[IN_VMEM] * len(arrays),
+        out_shape=[pltpu.VMEM(one.shape, one.dtype) for one in arrays],
+        scratch_shapes=[pltpu.SemaphoreType.DMA((len(arrays),))],
+        compiler_params=PARAMS,
+        name="preload",
+    )(*stay(*arrays))
+
+
+def padded(size):
+    return -(-size // 128) * 128
+
+
+def plane_call(received, potential, tables, bands, slots):
+    owners = len(received)
+    share, grid_side, _ = potential.shape
+    width = bands * 2 * slots
+    lane_pad = padded(grid_side // 2)
+    group = next(g for g in GROUPS if share % g == 0)
+    total = owners * slots
+    live = total // 2
+    return pl.pallas_call(
+        functools.partial(
+            plane_kernel, sources=owners, bands=bands, slots=slots, share=share, group=group
+        ),
+        in_specs=[IN_VMEM] * (owners + 5),
+        out_shape=[jax.ShapeDtypeStruct((share, width), BF16)] * owners,
+        scratch_shapes=[
+            pltpu.VMEM((2 * bands * received[0].shape[0], live), F32),
+            pltpu.VMEM((live, total), BF16),
+            pltpu.VMEM((grid_side // 4, live), F32),
+            pltpu.VMEM((live, 2 * lane_pad), BF16),
+            pltpu.VMEM((2 * lane_pad, live), BF16),
+            pltpu.VMEM((2 * bands * share, live), F32),
+        ],
+        compiler_params=PARAMS,
+        name="planes",
+    )(*received, potential, *tables)
+
+
 def body(coefficients, potential, stick_map, plane_order):
     bands, _, z_span, slots = coefficients.shape
     share, grid_side, _ = potential.shape
     owners = lax.axis_size("fft")
     width = bands * 2 * slots
-    lane_pad = -(-(grid_side // 2) // 128) * 128
     rows_sent = (share // 8 + 1) * 8
-    params = pltpu.CompilerParams(vmem_limit_bytes=48 << 20)
     me = lax.axis_index("fft").astype(jnp.int32).reshape(1)
-    in_smem = pl.BlockSpec(memory_space=pltpu.SMEM)
-    in_hbm = pl.BlockSpec(memory_space=pltpu.HBM)
-    in_vmem = pl.BlockSpec(memory_space=pltpu.VMEM)
-
-    def stay(*arrays):
-        return tuple(pltpu.with_memory_space_constraint(one, pltpu.HBM) for one in arrays)
 
     *sent, table, half_len = pl.pallas_call(
         functools.partial(stick_kernel, owners=owners, share=share),
-        in_specs=[in_smem] + [in_hbm] * 4,
+        in_specs=[IN_SMEM] + [IN_HBM] * 4,
         out_shape=[jax.ShapeDtypeStruct((rows_sent, width), BF16)] * owners
         + [
             jax.ShapeDtypeStruct((2 * z_span, grid_side), BF16),
@@ -325,7 +382,7 @@
             pltpu.VMEM((owners, share, width), BF16),
             pltpu.SemaphoreType.DMA((4,)),
         ],
-        compiler_params=params,
+        compiler_params=PARAMS,
         name="sticks",
     )(
         me,
@@ -334,39 +391,17 @@
         ),
     )
 
+    loaded = preload([potential, *axis_constants(grid_side, padded(grid_side // 2))])
     received = exchange(sent, owners, False)
 
-    group = next(g for g in (8, 4, 2, 1) if share % g == 0)
-    tables = axis_constants(grid_side, lane_pad)
-    total = owners * slots
-    columns = pl.pallas_call(
-        functools.partial(
-            plane_kernel, sources=owners, bands=bands, slots=slots, share=share, group=group
-        ),
-        in_specs=[in_vmem] * owners + [in_hbm] * 5,
-        out_shape=[jax.ShapeDtypeStruct((share, width), BF16)] * owners,
-        scratch_shapes=[pltpu.VMEM(potential.shape, F32)]
-        + [pltpu.VMEM(t.shape, BF16) for t in tables]
-        + [
-            pltpu.VMEM((owners, share, width), F32),
-            pltpu.VMEM((grid_side // 4, total), F32),
-            pltpu.VMEM((total, 2 * lane_pad), BF16),
-            pltpu.VMEM((2 * lane_pad, total), BF16),
-            pltpu.VMEM((owners, share, width), F32),
-            pltpu.SemaphoreType.DMA((4,)),
-            pltpu.SemaphoreType.DMA((share // group,)),
-        ],
-        compiler_params=params,
-        name="planes",
-    )(*received, *stay(potential, *tables))
-
+    columns = plane_call(received, loaded[0], loaded[1:], bands, slots)
     returned = exchange(columns, owners, True)
     return pl.pallas_call(
         functools.partial(column_kernel, owners=owners, slots=slots),
-        in_specs=[in_smem] + [in_vmem] * (owners + 2),
+        in_specs=[IN_SMEM] + [IN_VMEM] * (owners + 2),
         out_shape=jax.ShapeDtypeStruct(coefficients.shape, F32),
         scratch_shapes=[pltpu.VMEM((owners, share, width), BF16)],
-        compiler_params=params,
+        compiler_params=PARAMS,
         name="columns",
     )(me, half_len, table, *returned)
 

time: 38.1 us -> 34.1 us (0.90)
  waiting for transfers between devices: 7.68 us -> 4.37 us
  Pallas kernels: 20 us -> 19.3 us
    ppermute x6, waiting for transfers between devices: 7.68 us -> 4.37 us  [exchange(): result.append(lax.ppermute(part, 'fft', pairs))]
    pallas_call x1 -> x2, Pallas kernels: 17.5 us -> 16.8 us  [the longest x1 13 us: plane_call(): pl.pallas_call(functools.partial(plane_kernel, sources=owners, bands=band...]
  transfers between devices with their start and end apart: 6 -> 6, of which waited for: 4 -> 3; matrix products, arithmetic and copies ran while one was open for 0% -> 0% of each run, Pallas kernels for 0% -> 11%
where the time goes in v3:
time: 34.1 us; the launch traced here: 33.9 us
  Pallas kernels  19.3 us (57%)
  starting transfers between devices  10.2 us (30%)
  waiting for transfers between devices  4.37 us (13%)
    pallas_call x1, Pallas kernels, plane_call(): pl.pallas_call(functools.partial(plane_kernel, sources=owners, bands=band...  13 us
    ppermute x6, starting transfers between devices, exchange(): result.append(lax.ppermute(part, 'fft', pairs))  10.2 us
    ppermute x6, waiting for transfers between devices, exchange(): result.append(lax.ppermute(part, 'fft', pairs))  4.37 us
    pallas_call x1, Pallas kernels, preload(): pl.pallas_call(preload_kernel, in_specs=[IN_HBM] * len(arrays), out_specs...  3.84 us
    pallas_call x1, Pallas kernels, body(): pl.pallas_call(functools.partial(stick_kernel, owners=owners, share=share...  1.51 us
    pallas_call x1, Pallas kernels, body(): pl.pallas_call(functools.partial(column_kernel, owners=owners, slots=slot...  0.94 us
  transfers between devices with their start and end apart: 6, of which 3 were waited for; matrix products, arithmetic and copies ran while one was open for 0% of the time, Pallas kernels for 11%

profile of v3, /device:TPU:0, one launch (start us, length us, event | category | flops | bytes accessed | tf_op | source)
XLA Modules:
  0.0 33.9 jit_solution(16857598526924864993)
XLA Ops:
  0.0 1.5 %sticks.1 = (bf16[56,512]{1,0:T(8,128)(2,1)S(1)}, bf16[56,512]{1,0:T(8,128)(2,1)S(1)}, bf16[56,512]{1,0:T(8,128)(2,1)S(1)}, bf16[56,512]{1,0:T(8,128)(2,1)S(1)},...) custom-call(s32[1]{0:T(128)} %bitcast.me, bf16[1,2,128,256]{3,2,1,0:T(8,128)(2,1)} %coeff_h.1, s32[3,256]{1,0:T(4,128)} %smap_h.1, ...), custom_call_target="tpu_custom_call" | custom-call | tf_op jit(solution)/shard_map/sticks/pallas_call | solution.py:369
  1.5 5.1 %collective-permute-start = (bf16[56,512]{1,0:T(8,128)(2,1)S(1)}, bf16[56,512]{1,0:T(8,128)(2,1)S(1)}, u32[]{:S(2)}, u32[]{:S(2)}) collective-permute-start(bf16[56,512]{1,0:T(8,128)(2,1)S(1)} %get-tuple-element.23), channel_id=1, source_target_pairs={{0,12},{4,8},{8,4},{12,0},{1,13},{5,9},{9,5},{13,1},{2,14},{6,10},... | collective-permute-start | bytes 172040 | tf_op jit(solution)/shard_map/send3/ppermute | solution.py:308
  6.7 0.0 collective-permute-start.1
  6.7 0.6 %collective-permute-start.2 = (bf16[56,512]{1,0:T(8,128)(2,1)S(1)}, bf16[56,512]{1,0:T(8,128)(2,1)S(1)}, u32[]{:S(2)}, u32[]{:S(2)}) collective-permute-start(bf16[56,512]{1,0:T(8,128)(2,1)S(1)} %get-tuple-element.25), channel_id=1, source_target_pairs={{0,4},{4,0},{8,12},{12,8},{1,5},{5,1},{9,13},{13,9},{2,6},{6,2},{1... | collective-permute-start | bytes 172040 | tf_op jit(solution)/shard_map/send1/ppermute | solution.py:308
  7.3 3.8 %preload.1 = (f32[48,192,192]{2,1,0:T(8,128)S(1)}, bf16[384,192]{1,0:T(8,128)(2,1)S(1)}, bf16[2,256,192]{2,1,0:T(8,128)(2,1)S(1)}, bf16[2,192,256]{2,1,0:T(8,128)(2,1)S(1)}, bf16[2,192,192]{2,1,0:T(8,128)(2,1)S(1)}) custom-call(f32[48,192,192]{2,1,0:T(8,128)} %refs_0_.1, bf16[384,192]{1,0:T(8,128)(2,1)} %constant.16.clone.refs_1_, ...), custom_call_target="tpu_custom_call" | custom-call | tf_op jit(solution)/shard_map/preload/pallas_call | solution.py:319
  11.2 0.0 collective-permute-done.refs_1_
  11.2 0.6 %collective-permute-done.1.refs_2_ = bf16[56,512]{1,0:T(8,128)(2,1)S(1)} collective-permute-done((bf16[56,512]{1,0:T(8,128)(2,1)S(1)}, bf16[56,512]{1,0:T(8,128)(2,1)S(1)}, u32[]{:S(2)}, u32[]{:S(2)}) %collective-permute-start.1) | collective-permute-done | bytes 57376 | tf_op jit(solution)/shard_map/send2/ppermute | solution.py:308
  11.7 0.0 collective-permute-done.2.refs_3_
  11.7 13.0 %planes.1 = (bf16[48,512]{1,0:T(8,128)(2,1)S(1)}, bf16[48,512]{1,0:T(8,128)(2,1)S(1)}, bf16[48,512]{1,0:T(8,128)(2,1)S(1)}, bf16[48,512]{1,0:T(8,128)(2,1)S(1)}) custom-call(bf16[56,512]{1,0:T(8,128)(2,1)S(1)} %get-tuple-element.22.refs_0_, bf16[56,512]{1,0:T(8,128)(2,1)S(1)} %collective-permute-done.refs_1_, ...), custom_call_target="tpu_custom_call" | custom-call | tf_op jit(solution)/shard_map/planes/pallas_call | solution.py:342
  24.7 3.3 %collective-permute-start.3 = (bf16[48,512]{1,0:T(8,128)(2,1)S(1)}, bf16[48,512]{1,0:T(8,128)(2,1)S(1)}, u32[]{:S(2)}, u32[]{:S(2)}) collective-permute-start(bf16[48,512]{1,0:T(8,128)(2,1)S(1)} %get-tuple-element.32), channel_id=1, source_target_pairs={{12,0},{8,4},{4,8},{0,12},{13,1},{9,5},{5,9},{1,13},{14,2},{10,6},... | collective-permute-start | bytes 147464 | tf_op jit(solution)/shard_map/back3/ppermute | solution.py:308
  28.0 0.0 collective-permute-start.4
  28.0 1.2 %collective-permute-start.5 = (bf16[48,512]{1,0:T(8,128)(2,1)S(1)}, bf16[48,512]{1,0:T(8,128)(2,1)S(1)}, u32[]{:S(2)}, u32[]{:S(2)}) collective-permute-start(bf16[48,512]{1,0:T(8,128)(2,1)S(1)} %get-tuple-element.34), channel_id=1, source_target_pairs={{4,0},{0,4},{12,8},{8,12},{5,1},{1,5},{13,9},{9,13},{6,2},{2,6},{1... | collective-permute-start | bytes 147464 | tf_op jit(solution)/shard_map/back1/ppermute | solution.py:308
  29.2 1.5 %collective-permute-done.3.refs_1_ = bf16[48,512]{1,0:T(8,128)(2,1)S(1)} collective-permute-done((bf16[48,512]{1,0:T(8,128)(2,1)S(1)}, bf16[48,512]{1,0:T(8,128)(2,1)S(1)}, u32[]{:S(2)}, u32[]{:S(2)}) %collective-permute-start.3) | collective-permute-done | bytes 49184 | tf_op jit(solution)/shard_map/back3/ppermute | solution.py:308
  30.8 2.2 %collective-permute-done.4.refs_2_ = bf16[48,512]{1,0:T(8,128)(2,1)S(1)} collective-permute-done((bf16[48,512]{1,0:T(8,128)(2,1)S(1)}, bf16[48,512]{1,0:T(8,128)(2,1)S(1)}, u32[]{:S(2)}, u32[]{:S(2)}) %collective-permute-start.4) | collective-permute-done | bytes 49184 | tf_op jit(solution)/shard_map/back2/ppermute | solution.py:308
  33.0 0.0 collective-permute-done.5.refs_3_
  33.0 0.9 %columns.1 = f32[1,2,128,256]{3,2,1,0:T(8,128)} custom-call(s32[1]{0:T(128)} %bitcast.me, s32[8,256]{1,0:T(8,128)S(1)} %get-tuple-element.20.half_len, bf16[256,192]{1,0:T(8,128)(2,1)S(1)} %get-tuple-element.21.table, bf16[48,512]{1,0:T(8,128)(2,1)S(1)} %get-tuple-element.31.refs_0_, bf16[48,512]{1,0:T(8,128)(2,1)S(1)} %collective-permute-done.3.refs_1_, ...), custom_call_target="tpu_custom_call" | custom-call | tf_op jit(solution)/shard_map/columns/pallas_call | solution.py:399
Async XLA Ops:
  1.5 9.6 %collective-permute-start = (bf16[56,512]{1,0:T(8,128)(2,1)S(1)}, bf16[56,512]{1,0:T(8,128)(2,1)S(1)}, u32[]{:S(2)}, u32[]{:S(2)}) collective-permute-start(bf16[56,512]{1,0:T(8,128)(2,1)S(1)} %get-tuple-element.23), channel_id=1, source_target_pairs={{0,12},{4,8},{8,4},{12,0},{1,13},{5,9},{9,5},{13,1},{2,14},{6,10},... | collective-permute-start | bytes 172040 | tf_op jit(solution)/shard_map/send3/ppermute | solution.py:308
  6.7 5.1 %collective-permute-start.1 = (bf16[56,512]{1,0:T(8,128)(2,1)S(1)}, bf16[56,512]{1,0:T(8,128)(2,1)S(1)}, u32[]{:S(2)}, u32[]{:S(2)}) collective-permute-start(bf16[56,512]{1,0:T(8,128)(2,1)S(1)} %get-tuple-element.24), channel_id=1, source_target_pairs={{0,8},{4,12},{8,0},{12,4},{1,9},{5,13},{9,1},{13,5},{2,10},{6,14},... | collective-permute-start | bytes 172040 | tf_op jit(solution)/shard_map/send2/ppermute | solution.py:308
  6.7 5.1 %collective-permute-start.2 = (bf16[56,512]{1,0:T(8,128)(2,1)S(1)}, bf16[56,512]{1,0:T(8,128)(2,1)S(1)}, u32[]{:S(2)}, u32[]{:S(2)}) collective-permute-start(bf16[56,512]{1,0:T(8,128)(2,1)S(1)} %get-tuple-element.25), channel_id=1, source_target_pairs={{0,4},{4,0},{8,12},{12,8},{1,5},{5,1},{9,13},{13,9},{2,6},{6,2},{1... | collective-permute-start | bytes 172040 | tf_op jit(solution)/shard_map/send1/ppermute | solution.py:308
  24.7 6.0 %collective-permute-start.3 = (bf16[48,512]{1,0:T(8,128)(2,1)S(1)}, bf16[48,512]{1,0:T(8,128)(2,1)S(1)}, u32[]{:S(2)}, u32[]{:S(2)}) collective-permute-start(bf16[48,512]{1,0:T(8,128)(2,1)S(1)} %get-tuple-element.32), channel_id=1, source_target_pairs={{12,0},{8,4},{4,8},{0,12},{13,1},{9,5},{5,9},{1,13},{14,2},{10,6},... | collective-permute-start | bytes 147464 | tf_op jit(solution)/shard_map/back3/ppermute | solution.py:308
  28.0 5.0 %collective-permute-start.4 = (bf16[48,512]{1,0:T(8,128)(2,1)S(1)}, bf16[48,512]{1,0:T(8,128)(2,1)S(1)}, u32[]{:S(2)}, u32[]{:S(2)}) collective-permute-start(bf16[48,512]{1,0:T(8,128)(2,1)S(1)} %get-tuple-element.33), channel_id=1, source_target_pairs={{8,0},{12,4},{0,8},{4,12},{9,1},{13,5},{1,9},{5,13},{10,2},{14,6},... | collective-permute-start | bytes 147464 | tf_op jit(solution)/shard_map/back2/ppermute | solution.py:308
  28.0 5.0 %collective-permute-start.5 = (bf16[48,512]{1,0:T(8,128)(2,1)S(1)}, bf16[48,512]{1,0:T(8,128)(2,1)S(1)}, u32[]{:S(2)}, u32[]{:S(2)}) collective-permute-start(bf16[48,512]{1,0:T(8,128)(2,1)S(1)} %get-tuple-element.34), channel_id=1, source_target_pairs={{4,0},{0,4},{12,8},{8,12},{5,1},{1,5},{13,9},{9,13},{6,2},{2,6},{1... | collective-permute-start | bytes 147464 | tf_op jit(solution)/shard_map/back1/ppermute | solution.py:308

commit v4 on v3

--- a/solution.py
+++ b/solution.py
@@ -15,7 +15,7 @@
 IN_SMEM = pl.BlockSpec(memory_space=pltpu.SMEM)
 IN_HBM = pl.BlockSpec(memory_space=pltpu.HBM)
 IN_VMEM = pl.BlockSpec(memory_space=pltpu.VMEM)
-GROUPS = (8, 4, 2, 1)
+GROUPS = (48, 24, 16, 12, 8, 4, 2, 1)
 
 
 def stay(*arrays):
@@ -78,6 +78,13 @@
     return lax.dot_general(left, right, (((0,), (0,)), ((), ())), preferred_element_type=F32)
 
 
+def one_hot_columns(ids, count):
+    rows = lax.broadcasted_iota(jnp.int32, (count, ids.shape[1]), 0).astype(jnp.int16)
+    ids = jnp.broadcast_to(ids, (16, ids.shape[1])).astype(jnp.int16)
+    ids = jnp.concatenate([ids] * (count // 16), 0)
+    return jnp.where(rows == ids, jnp.ones((), BF16), jnp.zeros((), BF16))
+
+
 def hops(owners):
     return (0,) + tuple(range(owners - 1, 0, -1))
 
@@ -97,17 +104,14 @@
 
 def stick_kernel(me, coeff_h, smap_h, order_h, turn_h, *refs, owners, share):
     outs = refs[:owners]
-    table, half_len, coeff, smap, order, turn, sticks, sems = refs[owners:]
+    coeff, smap, order, turn, sticks, sems = refs[owners:]
     started = copies_in((order_h, turn_h, smap_h, coeff_h), (order, turn, smap, coeff), sems)
     bands, _, z_span, slots = coeff.shape
     grid_side = order.shape[1]
     started[0].wait()
-    chosen = lax.broadcasted_iota(jnp.int32, (grid_side, grid_side), 0) == order[...]
-    chosen = jnp.where(chosen, 1.0, 0.0).astype(BF16)
+    chosen = one_hot_columns(order[...], grid_side)
     started[1].wait()
-    rows = mm_t(chosen, turn[...])
-    table[...] = rows.T.astype(BF16)
-    rows = rows.astype(BF16)
+    rows = mm_t(chosen, turn[...]).astype(BF16)
     cos_rows, sin_rows = rows[:, :z_span], rows[:, z_span:]
     lefts = (
         jnp.concatenate([cos_rows, -sin_rows], 1),
@@ -116,7 +120,6 @@
     started[2].wait()
     entries = lax.broadcasted_iota(jnp.int32, (z_span, slots), 0)
     half = (smap[2:3, :] + 1) // 2 - 1
-    half_len[...] = jnp.broadcast_to(half, half_len.shape)
     keep = jnp.abs(entries - z_span // 2) <= half
     started[3].wait()
     for band in range(bands):
@@ -131,9 +134,21 @@
             for owner in range(owners):
                 sticks[owner, :, col : col + slots] = found[owner * share : (owner + 1) * share]
     spare = outs[0].shape[0] - share
-    x_id = jnp.where(half >= 0, smap[0:1, :], grid_side)
-    places = jnp.concatenate([x_id, smap[1:2, :]], 1).astype(F32)
-    places = jnp.broadcast_to(places, (spare, 2 * slots)).astype(BF16)
+    live = jnp.where(half >= 0, 1.0, 0.0)
+    upper = lax.broadcasted_iota(jnp.int32, (slots, slots), 0)
+    upper = upper < lax.broadcasted_iota(jnp.int32, (slots, slots), 1)
+    upper = jnp.where(upper, 1.0, 0.0).astype(BF16)
+    number = mm(jnp.broadcast_to(live, (8, slots)).astype(BF16), upper)[0:1]
+    number = jnp.where(half >= 0, number, -1.0)
+    count = jnp.broadcast_to(jnp.sum(live, axis=1, keepdims=True), (1, slots))
+    places = jnp.concatenate(
+        [
+            jnp.concatenate([smap[0:1, :], smap[1:2, :]], 1).astype(F32),
+            jnp.concatenate([number, count], 1),
+            jnp.zeros((spare - 2, 2 * slots), F32),
+        ],
+        0,
+    ).astype(BF16)
     for out, hop in zip(outs, hops(owners)):
         out[0:share, :] = sticks[partner(me[0], hop, owners)]
         out[share:, 0 : 2 * slots] = places
@@ -152,21 +167,15 @@
     lane_pad = high.shape[0] // 2
 
     live_count = low.shape[1]
-    upper = lax.broadcasted_iota(jnp.int32, (slots, slots), 0)
-    upper = upper < lax.broadcasted_iota(jnp.int32, (slots, slots), 1)
-    upper = jnp.where(upper, 1.0, 0.0).astype(BF16)
-    before = jnp.zeros((1, 1), F32)
+    before = jnp.zeros((1, slots), F32)
     gathered = None
     for src in range(sources):
         cols = slice(src * slots, (src + 1) * slots)
-        places = recv[src][share:, 0:slots].astype(F32)
-        live = jnp.where(places < grid_side, 1.0, 0.0)
-        rank = mm(live.astype(BF16), upper)[0:1] + before
-        live = live[0:1]
-        before = before + jnp.sum(live, axis=1, keepdims=True)
-        rank = jnp.where(live > 0.0, rank, -1.0).astype(jnp.int32)
-        numbers = lax.broadcasted_iota(jnp.int32, (live_count, slots), 0)
-        chosen = jnp.where(numbers == rank, 1.0, 0.0).astype(BF16)
+        places = recv[src][share:, :].astype(F32)
+        number = places[1:2, 0:slots]
+        number = jnp.where(number >= 0.0, number + before, -1.0)
+        before = before + places[1:2, slots : 2 * slots]
+        chosen = one_hot_columns(number.astype(jnp.int32), live_count)
         select[:, cols] = chosen
         pieces = [recv[src][:, i * slots : (i + 1) * slots] for i in range(2 * bands)]
         part = lax.dot_general(
@@ -186,10 +195,9 @@
     x_low = x_id - x_high * quarter
     rows = lax.broadcasted_iota(jnp.int32, (quarter, live_count), 0)
     low[...] = jnp.where(rows == x_low, 1.0, 0.0)
-    rows = lax.broadcasted_iota(jnp.int32, (2 * lane_pad, live_count), 0)
-    hot = jnp.where(rows == x_high * lane_pad + y_id, 1.0, 0.0)
-    high[...] = hot.astype(BF16)
-    high_t[...] = hot.T.astype(BF16)
+    hot = one_hot_columns(x_high * lane_pad + y_id, 2 * lane_pad)
+    high[...] = hot
+    high_t[...] = hot.T
 
     def one_group(step):
         base = step * group
@@ -264,9 +272,10 @@
         for pair, grid in zip(pairs, grids):
             pick(pair, grid)
 
-    @pl.loop(0, share // group)
-    def _(step):
-        one_group(step)
+    if group == share:
+        one_group(0)
+    else:
+        pl.loop(0, share // group)(one_group)
 
     spread_out = mm(acc[...].astype(BF16), select[...]).astype(BF16)
     for src in range(sources):
@@ -309,22 +318,36 @@
     return result
 
 
-def preload_kernel(*refs):
-    count = len(refs) // 2
-    for one in copies_in(refs[:count], refs[count : 2 * count], refs[2 * count]):
+def preload_kernel(order_h, turn_h, smap_h, *refs):
+    count = (len(refs) - 6) // 2
+    table, half_len, order, turn, smap, sems = refs[2 * count :]
+    started = copies_in(
+        (order_h, turn_h, smap_h, *refs[:count]), (order, turn, smap, *refs[count : 2 * count]), sems
+    )
+    for one in started[:3]:
         one.wait()
-
-
-def preload(arrays):
-    return pl.pallas_call(
+    chosen = one_hot_columns(order[...], order.shape[1])
+    table[...] = mm_t(turn[...], chosen).astype(BF16)
+    half = (smap[2:3, :] + 1) // 2 - 1
+    half_len[...] = jnp.broadcast_to(half, half_len.shape)
+    for one in started[3:]:
+        one.wait()
+
+
+def preload(order, turn, smap, arrays):
+    out = [(one.shape, one.dtype) for one in arrays]
+    out += [((turn.shape[1], order.shape[1]), BF16), ((8, smap.shape[1]), jnp.int32)]
+    *loaded, table, half_len = pl.pallas_call(
         preload_kernel,
-        in_specs=[IN_HBM] * len(arrays),
-        out_specs=[IN_VMEM] * len(arrays),
-        out_shape=[pltpu.VMEM(one.shape, one.dtype) for one in arrays],
-        scratch_shapes=[pltpu.SemaphoreType.DMA((len(arrays),))],
+        in_specs=[IN_HBM] * (len(arrays) + 3),
+        out_specs=[IN_VMEM] * len(out),
+        out_shape=[pltpu.VMEM(*one) for one in out],
+        scratch_shapes=[pltpu.VMEM(one.shape, one.dtype) for one in (order, turn, smap)]
+        + [pltpu.SemaphoreType.DMA((len(arrays) + 3,))],
         compiler_params=PARAMS,
         name="preload",
-    )(*stay(*arrays))
+    )(*stay(order, turn, smap, *arrays))
+    return loaded, table, half_len
 
 
 def padded(size):
@@ -363,35 +386,30 @@
     share, grid_side, _ = potential.shape
     owners = lax.axis_size("fft")
     width = bands * 2 * slots
-    rows_sent = (share // 8 + 1) * 8
+    rows_sent = -(-(share + 2) // 8) * 8
     me = lax.axis_index("fft").astype(jnp.int32).reshape(1)
 
-    *sent, table, half_len = pl.pallas_call(
+    order = plane_order.reshape(1, grid_side)
+    turn = z_constants(grid_side, z_span)
+
+    sent = pl.pallas_call(
         functools.partial(stick_kernel, owners=owners, share=share),
         in_specs=[IN_SMEM] + [IN_HBM] * 4,
-        out_shape=[jax.ShapeDtypeStruct((rows_sent, width), BF16)] * owners
-        + [
-            jax.ShapeDtypeStruct((2 * z_span, grid_side), BF16),
-            jax.ShapeDtypeStruct((8, slots), jnp.int32),
-        ],
+        out_shape=[jax.ShapeDtypeStruct((rows_sent, width), BF16)] * owners,
         scratch_shapes=[
             pltpu.VMEM(coefficients.shape, BF16),
             pltpu.VMEM(stick_map.shape, jnp.int32),
-            pltpu.VMEM((1, grid_side), jnp.int32),
-            pltpu.VMEM((grid_side, 2 * z_span), BF16),
+            pltpu.VMEM(order.shape, jnp.int32),
+            pltpu.VMEM(turn.shape, BF16),
             pltpu.VMEM((owners, share, width), BF16),
             pltpu.SemaphoreType.DMA((4,)),
         ],
         compiler_params=PARAMS,
         name="sticks",
-    )(
-        me,
-        *stay(
-            coefficients, stick_map, plane_order.reshape(1, grid_side), z_constants(grid_side, z_span)
-        ),
-    )
-
-    loaded = preload([potential, *axis_constants(grid_side, padded(grid_side // 2))])
+    )(me, *stay(coefficients, stick_map, order, turn))
+
+    axis_tables = axis_constants(grid_side, padded(grid_side // 2))
+    loaded, table, half_len = preload(order, turn, stick_map, [potential, *axis_tables])
     received = exchange(sent, owners, False)
 
     columns = plane_call(received, loaded[0], loaded[1:], bands, slots)

time: 34.1 us -> 31.9 us (0.935)
  Pallas kernels: 19.3 us -> 17.1 us
    pallas_call x1, Pallas kernels: 13 us -> 10.8 us  [plane_call(): pl.pallas_call(functools.partial(plane_kernel, sources=owners, bands=band...]
  transfers between devices with their start and end apart: 6 -> 6, of which waited for: 3 -> 3; matrix products, arithmetic and copies ran while one was open for 0% -> 0% of each run, Pallas kernels for 11% -> 12%
where the time goes in v4:
time: 31.9 us; the launch traced here: 31.8 us
  Pallas kernels  17.1 us (54%)
  starting transfers between devices  10.2 us (32%)
  waiting for transfers between devices  4.37 us (14%)
    pallas_call x1, Pallas kernels, plane_call(): pl.pallas_call(functools.partial(plane_kernel, sources=owners, bands=band...  10.8 us
    ppermute x6, starting transfers between devices, exchange(): result.append(lax.ppermute(part, 'fft', pairs))  10.2 us
    ppermute x6, waiting for transfers between devices, exchange(): result.append(lax.ppermute(part, 'fft', pairs))  4.37 us
    pallas_call x1, Pallas kernels, preload(): pl.pallas_call(preload_kernel, in_specs=[IN_HBM] * (len(arrays) + 3), out...  3.95 us
    pallas_call x1, Pallas kernels, body(): pl.pallas_call(functools.partial(stick_kernel, owners=owners, share=share...  1.4 us
    pallas_call x1, Pallas kernels, body(): pl.pallas_call(functools.partial(column_kernel, owners=owners, slots=slot...  0.95 us
  transfers between devices with their start and end apart: 6, of which 3 were waited for; matrix products, arithmetic and copies ran while one was open for 0% of the time, Pallas kernels for 12%

profile of v4, /device:TPU:0, one launch (start us, length us, event | category | flops | bytes accessed | tf_op | source)
XLA Modules:
  0.0 31.8 jit_solution(11668979789622057381)
XLA Ops:
  0.0 1.4 %sticks.1 = (bf16[56,512]{1,0:T(8,128)(2,1)S(1)}, bf16[56,512]{1,0:T(8,128)(2,1)S(1)}, bf16[56,512]{1,0:T(8,128)(2,1)S(1)}, bf16[56,512]{1,0:T(8,128)(2,1)S(1)}) custom-call(s32[1]{0:T(128)} %bitcast.me, bf16[1,2,128,256]{3,2,1,0:T(8,128)(2,1)} %coeff_h.1, s32[3,256]{1,0:T(4,128)} %smap_h.3, s32[1,192]{1,0:T(1,128)} %bitcast.2, ...), custom_call_target="tpu_custom_call" | custom-call | tf_op jit(solution)/shard_map/sticks/pallas_call | solution.py:395
  1.4 5.1 %collective-permute-start = (bf16[56,512]{1,0:T(8,128)(2,1)S(1)}, bf16[56,512]{1,0:T(8,128)(2,1)S(1)}, u32[]{:S(2)}, u32[]{:S(2)}) collective-permute-start(bf16[56,512]{1,0:T(8,128)(2,1)S(1)} %get-tuple-element.23), channel_id=1, source_target_pairs={{0,12},{4,8},{8,4},{12,0},{1,13},{5,9},{9,5},{13,1},{2,14},{6,10},... | collective-permute-start | bytes 172040 | tf_op jit(solution)/shard_map/send3/ppermute | solution.py:317
  6.5 0.0 collective-permute-start.1
  6.6 0.6 %collective-permute-start.2 = (bf16[56,512]{1,0:T(8,128)(2,1)S(1)}, bf16[56,512]{1,0:T(8,128)(2,1)S(1)}, u32[]{:S(2)}, u32[]{:S(2)}) collective-permute-start(bf16[56,512]{1,0:T(8,128)(2,1)S(1)} %get-tuple-element.25), channel_id=1, source_target_pairs={{0,4},{4,0},{8,12},{12,8},{1,5},{5,1},{9,13},{13,9},{2,6},{6,2},{1... | collective-permute-start | bytes 172040 | tf_op jit(solution)/shard_map/send1/ppermute | solution.py:317
  7.2 3.9 %preload.1 = (f32[48,192,192]{2,1,0:T(8,128)S(1)}, bf16[384,192]{1,0:T(8,128)(2,1)S(1)}, bf16[2,256,192]{2,1,0:T(8,128)(2,1)S(1)}, bf16[2,192,256]{2,1,0:T(8,128...) custom-call(s32[1,192]{1,0:T(1,128)} %bitcast.3, ...), custom_call_target="tpu_custom_call" | custom-call | tf_op jit(solution)/shard_map/preload/pallas_call | solution.py:340
  11.1 0.0 collective-permute-done.refs_1_
  11.2 0.5 %collective-permute-done.1.refs_2_ = bf16[56,512]{1,0:T(8,128)(2,1)S(1)} collective-permute-done((bf16[56,512]{1,0:T(8,128)(2,1)S(1)}, bf16[56,512]{1,0:T(8,128)(2,1)S(1)}, u32[]{:S(2)}, u32[]{:S(2)}) %collective-permute-start.1) | collective-permute-done | bytes 57376 | tf_op jit(solution)/shard_map/send2/ppermute | solution.py:317
  11.6 0.0 collective-permute-done.2.refs_3_
  11.6 10.8 %planes.1 = (bf16[48,512]{1,0:T(8,128)(2,1)S(1)}, bf16[48,512]{1,0:T(8,128)(2,1)S(1)}, bf16[48,512]{1,0:T(8,128)(2,1)S(1)}, bf16[48,512]{1,0:T(8,128)(2,1)S(1)}) custom-call(bf16[56,512]{1,0:T(8,128)(2,1)S(1)} %get-tuple-element.22.refs_0_, bf16[56,512]{1,0:T(8,128)(2,1)S(1)} %collective-permute-done.refs_1_, ...), custom_call_target="tpu_custom_call" | custom-call | tf_op jit(solution)/shard_map/planes/pallas_call | solution.py:365
  22.5 3.4 %collective-permute-start.3 = (bf16[48,512]{1,0:T(8,128)(2,1)S(1)}, bf16[48,512]{1,0:T(8,128)(2,1)S(1)}, u32[]{:S(2)}, u32[]{:S(2)}) collective-permute-start(bf16[48,512]{1,0:T(8,128)(2,1)S(1)} %get-tuple-element.32), channel_id=1, source_target_pairs={{12,0},{8,4},{4,8},{0,12},{13,1},{9,5},{5,9},{1,13},{14,2},{10,6},... | collective-permute-start | bytes 147464 | tf_op jit(solution)/shard_map/back3/ppermute | solution.py:317
  25.8 0.0 collective-permute-start.4
  25.8 1.1 %collective-permute-start.5 = (bf16[48,512]{1,0:T(8,128)(2,1)S(1)}, bf16[48,512]{1,0:T(8,128)(2,1)S(1)}, u32[]{:S(2)}, u32[]{:S(2)}) collective-permute-start(bf16[48,512]{1,0:T(8,128)(2,1)S(1)} %get-tuple-element.34), channel_id=1, source_target_pairs={{4,0},{0,4},{12,8},{8,12},{5,1},{1,5},{13,9},{9,13},{6,2},{2,6},{1... | collective-permute-start | bytes 147464 | tf_op jit(solution)/shard_map/back1/ppermute | solution.py:317
  26.9 1.5 %collective-permute-done.3.refs_1_ = bf16[48,512]{1,0:T(8,128)(2,1)S(1)} collective-permute-done((bf16[48,512]{1,0:T(8,128)(2,1)S(1)}, bf16[48,512]{1,0:T(8,128)(2,1)S(1)}, u32[]{:S(2)}, u32[]{:S(2)}) %collective-permute-start.3) | collective-permute-done | bytes 49184 | tf_op jit(solution)/shard_map/back3/ppermute | solution.py:317
  28.4 2.4 %collective-permute-done.4.refs_2_ = bf16[48,512]{1,0:T(8,128)(2,1)S(1)} collective-permute-done((bf16[48,512]{1,0:T(8,128)(2,1)S(1)}, bf16[48,512]{1,0:T(8,128)(2,1)S(1)}, u32[]{:S(2)}, u32[]{:S(2)}) %collective-permute-start.4) | collective-permute-done | bytes 49184 | tf_op jit(solution)/shard_map/back2/ppermute | solution.py:317
  30.8 0.0 collective-permute-done.5.refs_3_
  30.8 0.9 %columns.1 = f32[1,2,128,256]{3,2,1,0:T(8,128)} custom-call(s32[1]{0:T(128)} %bitcast.me, s32[8,256]{1,0:T(8,128)S(1)} %get-tuple-element.20.half_len, bf16[256,192]{1,0:T(8,128)(2,1)S(1)} %get-tuple-element.21.table, bf16[48,512]{1,0:T(8,128)(2,1)S(1)} %get-tuple-element.31.refs_0_, bf16[48,512]{1,0:T(8,128)(2,1)S(1)} %collective-permute-done.3.refs_1_, ...), custom_call_target="tpu_custom_call" | custom-call | tf_op jit(solution)/shard_map/columns/pallas_call | solution.py:417
Async XLA Ops:
  1.4 9.7 %collective-permute-start = (bf16[56,512]{1,0:T(8,128)(2,1)S(1)}, bf16[56,512]{1,0:T(8,128)(2,1)S(1)}, u32[]{:S(2)}, u32[]{:S(2)}) collective-permute-start(bf16[56,512]{1,0:T(8,128)(2,1)S(1)} %get-tuple-element.23), channel_id=1, source_target_pairs={{0,12},{4,8},{8,4},{12,0},{1,13},{5,9},{9,5},{13,1},{2,14},{6,10},... | collective-permute-start | bytes 172040 | tf_op jit(solution)/shard_map/send3/ppermute | solution.py:317
  6.5 5.1 %collective-permute-start.1 = (bf16[56,512]{1,0:T(8,128)(2,1)S(1)}, bf16[56,512]{1,0:T(8,128)(2,1)S(1)}, u32[]{:S(2)}, u32[]{:S(2)}) collective-permute-start(bf16[56,512]{1,0:T(8,128)(2,1)S(1)} %get-tuple-element.24), channel_id=1, source_target_pairs={{0,8},{4,12},{8,0},{12,4},{1,9},{5,13},{9,1},{13,5},{2,10},{6,14},... | collective-permute-start | bytes 172040 | tf_op jit(solution)/shard_map/send2/ppermute | solution.py:317
  6.6 5.1 %collective-permute-start.2 = (bf16[56,512]{1,0:T(8,128)(2,1)S(1)}, bf16[56,512]{1,0:T(8,128)(2,1)S(1)}, u32[]{:S(2)}, u32[]{:S(2)}) collective-permute-start(bf16[56,512]{1,0:T(8,128)(2,1)S(1)} %get-tuple-element.25), channel_id=1, source_target_pairs={{0,4},{4,0},{8,12},{12,8},{1,5},{5,1},{9,13},{13,9},{2,6},{6,2},{1... | collective-permute-start | bytes 172040 | tf_op jit(solution)/shard_map/send1/ppermute | solution.py:317
  22.5 6.0 %collective-permute-start.3 = (bf16[48,512]{1,0:T(8,128)(2,1)S(1)}, bf16[48,512]{1,0:T(8,128)(2,1)S(1)}, u32[]{:S(2)}, u32[]{:S(2)}) collective-permute-start(bf16[48,512]{1,0:T(8,128)(2,1)S(1)} %get-tuple-element.32), channel_id=1, source_target_pairs={{12,0},{8,4},{4,8},{0,12},{13,1},{9,5},{5,9},{1,13},{14,2},{10,6},... | collective-permute-start | bytes 147464 | tf_op jit(solution)/shard_map/back3/ppermute | solution.py:317
  25.8 5.0 %collective-permute-start.4 = (bf16[48,512]{1,0:T(8,128)(2,1)S(1)}, bf16[48,512]{1,0:T(8,128)(2,1)S(1)}, u32[]{:S(2)}, u32[]{:S(2)}) collective-permute-start(bf16[48,512]{1,0:T(8,128)(2,1)S(1)} %get-tuple-element.33), channel_id=1, source_target_pairs={{8,0},{12,4},{0,8},{4,12},{9,1},{13,5},{1,9},{5,13},{10,2},{14,6},... | collective-permute-start | bytes 147464 | tf_op jit(solution)/shard_map/back2/ppermute | solution.py:317
  25.8 5.0 %collective-permute-start.5 = (bf16[48,512]{1,0:T(8,128)(2,1)S(1)}, bf16[48,512]{1,0:T(8,128)(2,1)S(1)}, u32[]{:S(2)}, u32[]{:S(2)}) collective-permute-start(bf16[48,512]{1,0:T(8,128)(2,1)S(1)} %get-tuple-element.34), channel_id=1, source_target_pairs={{4,0},{0,4},{12,8},{8,12},{5,1},{1,5},{13,9},{9,13},{6,2},{2,6},{1... | collective-permute-start | bytes 147464 | tf_op jit(solution)/shard_map/back1/ppermute | solution.py:317

commit v5 on v4

--- a/solution.py
+++ b/solution.py
@@ -15,7 +15,7 @@
 IN_SMEM = pl.BlockSpec(memory_space=pltpu.SMEM)
 IN_HBM = pl.BlockSpec(memory_space=pltpu.HBM)
 IN_VMEM = pl.BlockSpec(memory_space=pltpu.VMEM)
-GROUPS = (48, 24, 16, 12, 8, 4, 2, 1)
+GROUPS = (24, 16, 12, 8, 4, 2)
 
 
 def stay(*arrays):
@@ -28,46 +28,32 @@
     return np.cos(angles), np.sin(angles)
 
 
-def pad_to(array, rows, cols):
-    return np.pad(array, ((0, rows - array.shape[0]), (0, cols - array.shape[1])))
-
-
 def z_constants(grid_side, z_span):
     freq = (np.arange(z_span) - z_span // 2) % grid_side
     return jnp.asarray(np.concatenate(angle_tables(np.arange(grid_side), freq, grid_side), 1), BF16)
 
 
-def axis_constants(grid_side, lane_pad):
+def axis_constants(grid_side, lane_pad, pair_pad):
     half = grid_side // 2
-    quarter = half // 2
-    grid_ids = np.arange(grid_side)
     compact = np.arange(half)
-    window = np.where(compact < quarter, compact, compact + half)
-    cos_w, sin_w = angle_tables(window, grid_ids, grid_side)
-
-    def by_high(top, bottom):
-        parts = []
-        for high in range(2):
-            rows = slice(high * quarter, (high + 1) * quarter)
-            parts += [top[rows], bottom[rows]]
-        return np.concatenate(parts, 0)
-
-    forward_x = np.concatenate([by_high(cos_w, -sin_w).T, by_high(sin_w, cos_w).T], 0)
-    pad = functools.partial(pad_to, rows=lane_pad, cols=grid_side)
-    forward_y = np.stack(
-        [
-            np.concatenate([pad(cos_w), pad(-sin_w)], 0),
-            np.concatenate([pad(sin_w), pad(cos_w)], 0),
-        ]
+    window = np.where(compact < half // 2, compact, compact + half)
+    cos_w, sin_w = angle_tables(window, np.arange(grid_side), grid_side)
+
+    def placed(table, phase):
+        spare = pair_pad - grid_side
+        lanes = (0, spare) if phase == 0 else (spare, 0)
+        return np.pad(table, ((0, lane_pad - half), lanes))
+
+    forward_y, inverse_y = [], []
+    for phase in range(2):
+        cos_p, sin_p = placed(cos_w, phase), placed(sin_w, phase)
+        forward_y.append([np.concatenate([cos_p, -sin_p], 0), np.concatenate([sin_p, cos_p], 0)])
+        inverse_y.append([np.concatenate([cos_p.T, -sin_p.T], 1), np.concatenate([sin_p.T, cos_p.T], 1)])
+    forward_x = np.concatenate(
+        [np.concatenate([cos_w.T, -sin_w.T], 1), np.concatenate([sin_w.T, cos_w.T], 1)], 0
     )
-    inverse_y = np.stack(
-        [
-            np.concatenate([pad(cos_w).T, pad(-sin_w).T], 1),
-            np.concatenate([pad(sin_w).T, pad(cos_w).T], 1),
-        ]
-    )
-    inverse_x = np.stack([by_high(cos_w, -sin_w), by_high(sin_w, cos_w)])
-    return tuple(jnp.asarray(t, BF16) for t in (forward_x, forward_y, inverse_y, inverse_x))
+    inverse_x = [np.concatenate([cos_w, -sin_w], 0), np.concatenate([sin_w, cos_w], 0)]
+    return tuple(jnp.asarray(np.array(t), BF16) for t in (forward_x, forward_y, inverse_y, inverse_x))
 
 
 def mm(left, right):
@@ -165,6 +151,8 @@
     half = grid_side // 2
     quarter = half // 2
     lane_pad = high.shape[0] // 2
+    pair_pad = fwd_y.shape[3]
+    overlap = 2 * grid_side - pair_pad
 
     live_count = low.shape[1]
     before = jnp.zeros((1, slots), F32)
@@ -201,76 +189,87 @@
 
     def one_group(step):
         base = step * group
-        units = [(plane, band) for plane in range(group) for band in range(bands)]
-        pairs = [units[i : i + 2] for i in range(0, len(units), 2)]
+        pairs = [((p, band), (p + 1, band)) for p in range(0, group, 2) for band in range(bands)]
+        bundles = [pairs[i : i + 2] for i in range(0, len(pairs), 2)]
         low_hot = low[...].astype(BF16)
 
-        def spread(pair):
+        def by_phase(bundle):
+            return [[pair[phase] for pair in bundle] for phase in range(2)]
+
+        def spread(units):
             stacked = []
-            for plane, band in pair:
+            for plane, band in units:
                 for comp in range(2):
                     row = vals[pl.ds((band * 2 + comp) * rows_sent + base + plane, 1), :]
                     stacked.append(jnp.broadcast_to(row, low_hot.shape).astype(BF16) * low_hot)
             spots = mm(jnp.concatenate(stacked, 0), high_t[...]).astype(BF16)
-            lanes = []
-            for i in range(len(pair)):
-                rows = spots[i * half : (i + 1) * half]
-                lanes.append(jnp.concatenate([rows[:, :lane_pad], rows[:, lane_pad:]], 0))
-            return jnp.concatenate(lanes, 1)
-
-        def along_x(grid):
-            return mm(fwd_x[...], grid).astype(BF16)
-
-        def along_y(grid):
+            rows = []
+            for i in range(len(units)):
+                real = spots[i * half : i * half + quarter]
+                imag = spots[i * half + quarter : (i + 1) * half]
+                for lanes in (slice(0, lane_pad), slice(lane_pad, 2 * lane_pad)):
+                    rows.append(jnp.concatenate([real[:, lanes], imag[:, lanes]], 1))
+            return jnp.concatenate(rows, 0)
+
+        def along_y(grids):
+            parts = []
+            for comp in range(2):
+                found = [mm(grid, fwd_y[phase, comp]).astype(BF16) for phase, grid in enumerate(grids)]
+                lanes = []
+                for i in range(found[0].shape[0] // half):
+                    first, second = (one[i * half : (i + 1) * half] for one in found)
+                    lanes += [first[:, :overlap], first[:, overlap:] + second[:, :-overlap]]
+                    lanes.append(second[:, -overlap:])
+                parts.append(jnp.concatenate(lanes, 1))
+            return jnp.concatenate(parts, 0)
+
+        def along_x(bundle, grid):
+            fields = mm(fwd_x[...], grid)
+            field = jnp.concatenate([pot[base + plane] for pair in bundle for plane, _ in pair], 1)
+            return [
+                (fields[comp * grid_side : (comp + 1) * grid_side] * field).astype(BF16)
+                for comp in range(2)
+            ]
+
+        def back_x(product):
+            return (mm(inv_x[0], product[0]) + mm(inv_x[1], product[1])).astype(BF16)
+
+        def back_y(grid, count):
+            result = []
+            for phase in range(2):
+                total = None
+                for comp in range(2):
+                    rows = []
+                    for i in range(count):
+                        start = i * 2 * grid_side + phase * overlap
+                        rows.append(grid[comp * half : (comp + 1) * half, start : start + pair_pad])
+                    part = mm(jnp.concatenate(rows, 0), inv_y[phase, comp])
+                    total = part if total is None else total + part
+                result.append(total.astype(BF16))
+            return result
+
+        def pick(units, grid):
             stacked = []
-            for i in range(grid.shape[1] // lane_pad):
-                cols = slice(i * lane_pad, (i + 1) * lane_pad)
-                stacked.append(jnp.concatenate([grid[:grid_side, cols], grid[grid_side:, cols]], 1))
-            stacked = jnp.concatenate(stacked, 0)
-            return mm(stacked, fwd_y[0]), mm(stacked, fwd_y[1])
-
-        def times_potential(pair, fields):
-            real, imag = [], []
-            for i, (plane, _) in enumerate(pair):
-                rows = slice(i * grid_side, (i + 1) * grid_side)
-                field = pot[base + plane]
-                real.append((fields[0][rows] * field).astype(BF16))
-                imag.append((fields[1][rows] * field).astype(BF16))
-            return jnp.concatenate(real, 0), jnp.concatenate(imag, 0)
-
-        def back_y(product):
-            return (mm(product[0], inv_y[0]) + mm(product[1], inv_y[1])).astype(BF16)
-
-        def back_x(grid):
-            count = grid.shape[0] // grid_side
-            total = None
-            for comp in range(2):
-                cols = slice(comp * lane_pad, (comp + 1) * lane_pad)
-                rhs = [grid[i * grid_side : (i + 1) * grid_side, cols] for i in range(count)]
-                part = mm(inv_x[comp], jnp.concatenate(rhs, 1))
-                total = part if total is None else total + part
-            return total.astype(BF16)
-
-        def pick(pair, grid):
-            stacked = []
-            for i in range(len(pair)):
-                cols = slice(i * lane_pad, (i + 1) * lane_pad)
-                stacked.append(jnp.concatenate([grid[:half, cols], grid[half:, cols]], 1))
+            for i in range(len(units)):
+                top = grid[i * half : i * half + quarter]
+                bottom = grid[i * half + quarter : (i + 1) * half]
+                for lanes in (slice(0, lane_pad), slice(lane_pad, 2 * lane_pad)):
+                    stacked.append(jnp.concatenate([top[:, lanes], bottom[:, lanes]], 1))
             found = mm(jnp.concatenate(stacked, 0), high[...])
-            for i, (plane, band) in enumerate(pair):
+            for i, (plane, band) in enumerate(units):
                 for comp in range(2):
                     start = i * half + comp * quarter
                     line = jnp.sum(found[start : start + quarter] * low[...], axis=0, keepdims=True)
                     acc[pl.ds((band * 2 + comp) * share + base + plane, 1), :] = line
 
-        grids = [spread(pair) for pair in pairs]
-        grids = [along_x(grid) for grid in grids]
-        fields = [along_y(grid) for grid in grids]
-        products = [times_potential(pair, field) for pair, field in zip(pairs, fields)]
-        grids = [back_y(product) for product in products]
-        grids = [back_x(grid) for grid in grids]
-        for pair, grid in zip(pairs, grids):
-            pick(pair, grid)
+        grids = [[spread(units) for units in by_phase(bundle)] for bundle in bundles]
+        grids = [along_y(grid) for grid in grids]
+        products = [along_x(bundle, grid) for bundle, grid in zip(bundles, grids)]
+        grids = [back_x(product) for product in products]
+        grids = [back_y(grid, len(bundle)) for bundle, grid in zip(bundles, grids)]
+        for bundle, grid in zip(bundles, grids):
+            for units, part in zip(by_phase(bundle), grid):
+                pick(units, part)
 
     if group == share:
         one_group(0)
@@ -408,8 +407,8 @@
         name="sticks",
     )(me, *stay(coefficients, stick_map, order, turn))
 
-    axis_tables = axis_constants(grid_side, padded(grid_side // 2))
-    loaded, table, half_len = preload(order, turn, stick_map, [potential, *axis_tables])
+    tables = axis_constants(grid_side, padded(grid_side // 2), padded(grid_side))
+    loaded, table, half_len = preload(order, turn, stick_map, [potential, *tables])
     received = exchange(sent, owners, False)
 
     columns = plane_call(received, loaded[0], loaded[1:], bands, slots)

time: 31.9 us -> 31.3 us (0.981)
  Pallas kernels: 17.1 us -> 16.5 us
    pallas_call x1, Pallas kernels: 10.8 us -> 10 us  [plane_call(): pl.pallas_call(functools.partial(plane_kernel, sources=owners, bands=band...]
  transfers between devices with their start and end apart: 6 -> 6, of which waited for: 3 -> 3; matrix products, arithmetic and copies ran while one was open for 0% -> 0% of each run, Pallas kernels for 12% -> 13%
where the time goes in v5:
time: 31.3 us; the launch traced here: 31.1 us
  Pallas kernels  16.5 us (53%)
  starting transfers between devices  10.2 us (33%)
  waiting for transfers between devices  4.38 us (14%)
    ppermute x6, starting transfers between devices, exchange(): result.append(lax.ppermute(part, 'fft', pairs))  10.2 us
    pallas_call x1, Pallas kernels, plane_call(): pl.pallas_call(functools.partial(plane_kernel, sources=owners, bands=band...  10 us
    ppermute x6, waiting for transfers between devices, exchange(): result.append(lax.ppermute(part, 'fft', pairs))  4.38 us
    pallas_call x1, Pallas kernels, preload(): pl.pallas_call(preload_kernel, in_specs=[IN_HBM] * (len(arrays) + 3), out...  4.12 us
    pallas_call x1, Pallas kernels, body(): pl.pallas_call(functools.partial(stick_kernel, owners=owners, share=share...  1.4 us
    pallas_call x1, Pallas kernels, body(): pl.pallas_call(functools.partial(column_kernel, owners=owners, slots=slot...  0.95 us
  transfers between devices with their start and end apart: 6, of which 3 were waited for; matrix products, arithmetic and copies ran while one was open for 0% of the time, Pallas kernels for 13%

profile of v5, /device:TPU:0, one launch (start us, length us, event | category | flops | bytes accessed | tf_op | source)
XLA Modules:
  0.0 31.1 jit_solution(2116071766203246438)
XLA Ops:
  0.0 1.4 %sticks.1 = (bf16[56,512]{1,0:T(8,128)(2,1)S(1)}, bf16[56,512]{1,0:T(8,128)(2,1)S(1)}, bf16[56,512]{1,0:T(8,128)(2,1)S(1)}, bf16[56,512]{1,0:T(8,128)(2,1)S(1)}) custom-call(s32[1]{0:T(128)} %bitcast.me, bf16[1,2,128,256]{3,2,1,0:T(8,128)(2,1)} %coeff_h.1, s32[3,256]{1,0:T(4,128)} %smap_h.3, s32[1,192]{1,0:T(1,128)} %bitcast.2, ...), custom_call_target="tpu_custom_call" | custom-call | tf_op jit(solution)/shard_map/sticks/pallas_call | solution.py:394
  1.4 5.1 %collective-permute-start = (bf16[56,512]{1,0:T(8,128)(2,1)S(1)}, bf16[56,512]{1,0:T(8,128)(2,1)S(1)}, u32[]{:S(2)}, u32[]{:S(2)}) collective-permute-start(bf16[56,512]{1,0:T(8,128)(2,1)S(1)} %get-tuple-element.23), channel_id=1, source_target_pairs={{0,12},{4,8},{8,4},{12,0},{1,13},{5,9},{9,5},{13,1},{2,14},{6,10},... | collective-permute-start | bytes 172040 | tf_op jit(solution)/shard_map/send3/ppermute | solution.py:316
  6.5 0.0 collective-permute-start.1
  6.6 0.6 %collective-permute-start.2 = (bf16[56,512]{1,0:T(8,128)(2,1)S(1)}, bf16[56,512]{1,0:T(8,128)(2,1)S(1)}, u32[]{:S(2)}, u32[]{:S(2)}) collective-permute-start(bf16[56,512]{1,0:T(8,128)(2,1)S(1)} %get-tuple-element.25), channel_id=1, source_target_pairs={{0,4},{4,0},{8,12},{12,8},{1,5},{5,1},{9,13},{13,9},{2,6},{6,2},{1... | collective-permute-start | bytes 172040 | tf_op jit(solution)/shard_map/send1/ppermute | solution.py:316
  7.2 4.1 %preload.1 = (f32[48,192,192]{2,1,0:T(8,128)S(1)}, bf16[384,192]{1,0:T(8,128)(2,1)S(1)}, bf16[2,2,256,256]{3,2,1,0:T(8,128)(2,1)S(1)}, bf16[2,2,256,256]{3,2,1,0...) custom-call(s32[1,192]{1,0:T(1,128)} %bitcast.3, ...), custom_call_target="tpu_custom_call" | custom-call | tf_op jit(solution)/shard_map/preload/pallas_call | solution.py:339
  11.3 0.0 collective-permute-done.refs_1_
  11.3 0.3 collective-permute-done.1.refs_2_
  11.6 0.0 collective-permute-done.2.refs_3_
  11.6 10.0 %planes.1 = (bf16[48,512]{1,0:T(8,128)(2,1)S(1)}, bf16[48,512]{1,0:T(8,128)(2,1)S(1)}, bf16[48,512]{1,0:T(8,128)(2,1)S(1)}, bf16[48,512]{1,0:T(8,128)(2,1)S(1)}) custom-call(bf16[56,512]{1,0:T(8,128)(2,1)S(1)} %get-tuple-element.22.refs_0_, bf16[56,512]{1,0:T(8,128)(2,1)S(1)} %collective-permute-done.refs_1_, ...), custom_call_target="tpu_custom_call" | custom-call | tf_op jit(solution)/shard_map/planes/pallas_call | solution.py:364
  21.6 3.5 %collective-permute-start.3 = (bf16[48,512]{1,0:T(8,128)(2,1)S(1)}, bf16[48,512]{1,0:T(8,128)(2,1)S(1)}, u32[]{:S(2)}, u32[]{:S(2)}) collective-permute-start(bf16[48,512]{1,0:T(8,128)(2,1)S(1)} %get-tuple-element.32), channel_id=1, source_target_pairs={{12,0},{8,4},{4,8},{0,12},{13,1},{9,5},{5,9},{1,13},{14,2},{10,6},... | collective-permute-start | bytes 147464 | tf_op jit(solution)/shard_map/back3/ppermute | solution.py:316
  25.2 0.0 collective-permute-start.4
  25.2 0.9 %collective-permute-start.5 = (bf16[48,512]{1,0:T(8,128)(2,1)S(1)}, bf16[48,512]{1,0:T(8,128)(2,1)S(1)}, u32[]{:S(2)}, u32[]{:S(2)}) collective-permute-start(bf16[48,512]{1,0:T(8,128)(2,1)S(1)} %get-tuple-element.34), channel_id=1, source_target_pairs={{4,0},{0,4},{12,8},{8,12},{5,1},{1,5},{13,9},{9,13},{6,2},{2,6},{1... | collective-permute-start | bytes 147464 | tf_op jit(solution)/shard_map/back1/ppermute | solution.py:316
  26.1 1.5 %collective-permute-done.3.refs_1_ = bf16[48,512]{1,0:T(8,128)(2,1)S(1)} collective-permute-done((bf16[48,512]{1,0:T(8,128)(2,1)S(1)}, bf16[48,512]{1,0:T(8,128)(2,1)S(1)}, u32[]{:S(2)}, u32[]{:S(2)}) %collective-permute-start.3) | collective-permute-done | bytes 49184 | tf_op jit(solution)/shard_map/back3/ppermute | solution.py:316
  27.6 2.6 %collective-permute-done.4.refs_2_ = bf16[48,512]{1,0:T(8,128)(2,1)S(1)} collective-permute-done((bf16[48,512]{1,0:T(8,128)(2,1)S(1)}, bf16[48,512]{1,0:T(8,128)(2,1)S(1)}, u32[]{:S(2)}, u32[]{:S(2)}) %collective-permute-start.4) | collective-permute-done | bytes 49184 | tf_op jit(solution)/shard_map/back2/ppermute | solution.py:316
  30.2 0.0 collective-permute-done.5.refs_3_
  30.2 0.9 %columns.1 = f32[1,2,128,256]{3,2,1,0:T(8,128)} custom-call(s32[1]{0:T(128)} %bitcast.me, s32[8,256]{1,0:T(8,128)S(1)} %get-tuple-element.20.half_len, bf16[256,192]{1,0:T(8,128)(2,1)S(1)} %get-tuple-element.21.table, bf16[48,512]{1,0:T(8,128)(2,1)S(1)} %get-tuple-element.31.refs_0_, bf16[48,512]{1,0:T(8,128)(2,1)S(1)} %collective-permute-done.3.refs_1_, ...), custom_call_target="tpu_custom_call" | custom-call | tf_op jit(solution)/shard_map/columns/pallas_call | solution.py:416
Async XLA Ops:
  1.4 9.9 %collective-permute-start = (bf16[56,512]{1,0:T(8,128)(2,1)S(1)}, bf16[56,512]{1,0:T(8,128)(2,1)S(1)}, u32[]{:S(2)}, u32[]{:S(2)}) collective-permute-start(bf16[56,512]{1,0:T(8,128)(2,1)S(1)} %get-tuple-element.23), channel_id=1, source_target_pairs={{0,12},{4,8},{8,4},{12,0},{1,13},{5,9},{9,5},{13,1},{2,14},{6,10},... | collective-permute-start | bytes 172040 | tf_op jit(solution)/shard_map/send3/ppermute | solution.py:316
  6.5 5.1 %collective-permute-start.1 = (bf16[56,512]{1,0:T(8,128)(2,1)S(1)}, bf16[56,512]{1,0:T(8,128)(2,1)S(1)}, u32[]{:S(2)}, u32[]{:S(2)}) collective-permute-start(bf16[56,512]{1,0:T(8,128)(2,1)S(1)} %get-tuple-element.24), channel_id=1, source_target_pairs={{0,8},{4,12},{8,0},{12,4},{1,9},{5,13},{9,1},{13,5},{2,10},{6,14},... | collective-permute-start | bytes 172040 | tf_op jit(solution)/shard_map/send2/ppermute | solution.py:316
  6.6 5.1 %collective-permute-start.2 = (bf16[56,512]{1,0:T(8,128)(2,1)S(1)}, bf16[56,512]{1,0:T(8,128)(2,1)S(1)}, u32[]{:S(2)}, u32[]{:S(2)}) collective-permute-start(bf16[56,512]{1,0:T(8,128)(2,1)S(1)} %get-tuple-element.25), channel_id=1, source_target_pairs={{0,4},{4,0},{8,12},{12,8},{1,5},{5,1},{9,13},{13,9},{2,6},{6,2},{1... | collective-permute-start | bytes 172040 | tf_op jit(solution)/shard_map/send1/ppermute | solution.py:316
  21.6 6.0 %collective-permute-start.3 = (bf16[48,512]{1,0:T(8,128)(2,1)S(1)}, bf16[48,512]{1,0:T(8,128)(2,1)S(1)}, u32[]{:S(2)}, u32[]{:S(2)}) collective-permute-start(bf16[48,512]{1,0:T(8,128)(2,1)S(1)} %get-tuple-element.32), channel_id=1, source_target_pairs={{12,0},{8,4},{4,8},{0,12},{13,1},{9,5},{5,9},{1,13},{14,2},{10,6},... | collective-permute-start | bytes 147464 | tf_op jit(solution)/shard_map/back3/ppermute | solution.py:316
  25.2 5.0 %collective-permute-start.4 = (bf16[48,512]{1,0:T(8,128)(2,1)S(1)}, bf16[48,512]{1,0:T(8,128)(2,1)S(1)}, u32[]{:S(2)}, u32[]{:S(2)}) collective-permute-start(bf16[48,512]{1,0:T(8,128)(2,1)S(1)} %get-tuple-element.33), channel_id=1, source_target_pairs={{8,0},{12,4},{0,8},{4,12},{9,1},{13,5},{1,9},{5,13},{10,2},{14,6},... | collective-permute-start | bytes 147464 | tf_op jit(solution)/shard_map/back2/ppermute | solution.py:316
  25.2 5.0 %collective-permute-start.5 = (bf16[48,512]{1,0:T(8,128)(2,1)S(1)}, bf16[48,512]{1,0:T(8,128)(2,1)S(1)}, u32[]{:S(2)}, u32[]{:S(2)}) collective-permute-start(bf16[48,512]{1,0:T(8,128)(2,1)S(1)} %get-tuple-element.34), channel_id=1, source_target_pairs={{4,0},{0,4},{12,8},{8,12},{5,1},{1,5},{13,9},{9,13},{6,2},{2,6},{1... | collective-permute-start | bytes 147464 | tf_op jit(solution)/shard_map/back1/ppermute | solution.py:316

commit v6 on v5

--- a/solution.py
+++ b/solution.py
@@ -144,10 +144,18 @@
 
 def plane_kernel(*refs, sources, bands, slots, share, group):
     recv = refs[:sources]
-    pot, fwd_x, fwd_y, inv_y, inv_x = refs[sources : sources + 5]
-    outs = refs[sources + 5 : 2 * sources + 5]
-    vals, select, low, high_t, high, acc = refs[2 * sources + 5 :]
-    grid_side = pot.shape[1]
+    pot_h, pot_first, fwd_x, fwd_y, inv_y, inv_x = refs[sources : sources + 6]
+    outs = refs[sources + 6 : 2 * sources + 6]
+    vals, select, low, high_t, high, acc, pot_later, sems = refs[2 * sources + 6 :]
+    grid_side = pot_first.shape[1]
+    steps = share // group
+
+    def pot_copy(step):
+        rows = pl.ds(step * group, group)
+        return pltpu.make_async_copy(pot_h.at[rows], pot_later.at[step - 1], sems.at[step - 1])
+
+    for step in range(1, steps):
+        pot_copy(step).start()
     half = grid_side // 2
     quarter = half // 2
     lane_pad = high.shape[0] // 2
@@ -189,6 +197,7 @@
 
     def one_group(step):
         base = step * group
+        pot = pot_first if step == 0 else pot_later.at[step - 1]
         pairs = [((p, band), (p + 1, band)) for p in range(0, group, 2) for band in range(bands)]
         bundles = [pairs[i : i + 2] for i in range(0, len(pairs), 2)]
         low_hot = low[...].astype(BF16)
@@ -225,7 +234,7 @@
 
         def along_x(bundle, grid):
             fields = mm(fwd_x[...], grid)
-            field = jnp.concatenate([pot[base + plane] for pair in bundle for plane, _ in pair], 1)
+            field = jnp.concatenate([pot[plane] for pair in bundle for plane, _ in pair], 1)
             return [
                 (fields[comp * grid_side : (comp + 1) * grid_side] * field).astype(BF16)
                 for comp in range(2)
@@ -271,10 +280,10 @@
             for units, part in zip(by_phase(bundle), grid):
                 pick(units, part)
 
-    if group == share:
-        one_group(0)
-    else:
-        pl.loop(0, share // group)(one_group)
+    for step in range(steps):
+        if step > 0:
+            pot_copy(step).wait()
+        one_group(step)
 
     spread_out = mm(acc[...].astype(BF16), select[...]).astype(BF16)
     for src in range(sources):
@@ -320,8 +329,12 @@
 def preload_kernel(order_h, turn_h, smap_h, *refs):
     count = (len(refs) - 6) // 2
     table, half_len, order, turn, smap, sems = refs[2 * count :]
+    wanted = [
+        one.at[pl.ds(0, target.shape[0])] if one.shape != target.shape else one
+        for one, target in zip(refs[:count], refs[count : 2 * count])
+    ]
     started = copies_in(
-        (order_h, turn_h, smap_h, *refs[:count]), (order, turn, smap, *refs[count : 2 * count]), sems
+        (order_h, turn_h, smap_h, *wanted), (order, turn, smap, *refs[count : 2 * count]), sems
     )
     for one in started[:3]:
         one.wait()
@@ -333,8 +346,10 @@
         one.wait()
 
 
-def preload(order, turn, smap, arrays):
-    out = [(one.shape, one.dtype) for one in arrays]
+def preload(order, turn, smap, potential, tables):
+    arrays = [potential, *tables]
+    out = [((group_size(potential.shape[0]),) + potential.shape[1:], F32)]
+    out += [(one.shape, one.dtype) for one in tables]
     out += [((turn.shape[1], order.shape[1]), BF16), ((8, smap.shape[1]), jnp.int32)]
     *loaded, table, half_len = pl.pallas_call(
         preload_kernel,
@@ -353,19 +368,24 @@
     return -(-size // 128) * 128
 
 
-def plane_call(received, potential, tables, bands, slots):
+def group_size(share):
+    return next(g for g in GROUPS if share % g == 0)
+
+
+def plane_call(received, potential, pot_first, tables, bands, slots):
     owners = len(received)
     share, grid_side, _ = potential.shape
     width = bands * 2 * slots
     lane_pad = padded(grid_side // 2)
-    group = next(g for g in GROUPS if share % g == 0)
+    group = group_size(share)
+    later = max(share // group - 1, 1)
     total = owners * slots
     live = total // 2
     return pl.pallas_call(
         functools.partial(
             plane_kernel, sources=owners, bands=bands, slots=slots, share=share, group=group
         ),
-        in_specs=[IN_VMEM] * (owners + 5),
+        in_specs=[IN_VMEM] * owners + [IN_HBM] + [IN_VMEM] * 5,
         out_shape=[jax.ShapeDtypeStruct((share, width), BF16)] * owners,
         scratch_shapes=[
             pltpu.VMEM((2 * bands * received[0].shape[0], live), F32),
@@ -374,10 +394,12 @@
             pltpu.VMEM((live, 2 * lane_pad), BF16),
             pltpu.VMEM((2 * lane_pad, live), BF16),
             pltpu.VMEM((2 * bands * share, live), F32),
+            pltpu.VMEM((later, group, grid_side, grid_side), F32),
+            pltpu.SemaphoreType.DMA((later,)),
         ],
         compiler_params=PARAMS,
         name="planes",
-    )(*received, potential, *tables)
+    )(*received, *stay(potential), pot_first, *tables)
 
 
 def body(coefficients, potential, stick_map, plane_order):
@@ -408,10 +430,10 @@
     )(me, *stay(coefficients, stick_map, order, turn))
 
     tables = axis_constants(grid_side, padded(grid_side // 2), padded(grid_side))
-    loaded, table, half_len = preload(order, turn, stick_map, [potential, *tables])
+    loaded, table, half_len = preload(order, turn, stick_map, potential, tables)
     received = exchange(sent, owners, False)
 
-    columns = plane_call(received, loaded[0], loaded[1:], bands, slots)
+    columns = plane_call(received, potential, loaded[0], loaded[1:], bands, slots)
     returned = exchange(columns, owners, True)
     return pl.pallas_call(
         functools.partial(column_kernel, owners=owners, slots=slots),

time: 31.3 us -> 30.8 us (0.984)
  Pallas kernels: 16.5 us -> 15.5 us
  waiting for transfers between devices: 4.38 us -> 4.8 us
    pallas_call x1, Pallas kernels: 4.12 us -> 2.86 us  [preload(): pl.pallas_call(preload_kernel, in_specs=[IN_HBM] * (len(arrays) + 3), out...]
    ppermute x6, waiting for transfers between devices: 4.38 us -> 4.8 us  [exchange(): result.append(lax.ppermute(part, 'fft', pairs))]
    pallas_call x1, Pallas kernels: 10 us -> 10.3 us  [plane_call(): pl.pallas_call(functools.partial(plane_kernel, sources=owners, bands=band...]
  transfers between devices with their start and end apart: 6 -> 6, of which waited for: 3 -> 3; matrix products, arithmetic and copies ran while one was open for 0% -> 0% of each run, Pallas kernels for 13% -> 9%
where the time goes in v6:
time: 30.8 us; the launch traced here: 30.6 us
  Pallas kernels  15.5 us (50%)
  starting transfers between devices  10.2 us (33%)
  waiting for transfers between devices  4.8 us (16%)
    pallas_call x1, Pallas kernels, plane_call(): pl.pallas_call(functools.partial(plane_kernel, sources=owners, bands=band...  10.3 us
    ppermute x6, starting transfers between devices, exchange(): result.append(lax.ppermute(part, 'fft', pairs))  10.2 us
    ppermute x6, waiting for transfers between devices, exchange(): result.append(lax.ppermute(part, 'fft', pairs))  4.8 us
    pallas_call x1, Pallas kernels, preload(): pl.pallas_call(preload_kernel, in_specs=[IN_HBM] * (len(arrays) + 3), out...  2.86 us
    pallas_call x1, Pallas kernels, body(): pl.pallas_call(functools.partial(stick_kernel, owners=owners, share=share...  1.4 us
    pallas_call x1, Pallas kernels, body(): pl.pallas_call(functools.partial(column_kernel, owners=owners, slots=slot...  0.95 us
  transfers between devices with their start and end apart: 6, of which 3 were waited for; matrix products, arithmetic and copies ran while one was open for 0% of the time, Pallas kernels for 9%

profile of v6, /device:TPU:0, one launch (start us, length us, event | category | flops | bytes accessed | tf_op | source)
XLA Modules:
  0.0 30.6 jit_solution(1360330344607951154)
XLA Ops:
  0.0 1.4 %sticks.1 = (bf16[56,512]{1,0:T(8,128)(2,1)S(1)}, bf16[56,512]{1,0:T(8,128)(2,1)S(1)}, bf16[56,512]{1,0:T(8,128)(2,1)S(1)}, bf16[56,512]{1,0:T(8,128)(2,1)S(1)}) custom-call(s32[1]{0:T(128)} %bitcast.me, bf16[1,2,128,256]{3,2,1,0:T(8,128)(2,1)} %coeff_h.1, s32[3,256]{1,0:T(4,128)} %smap_h.3, s32[1,192]{1,0:T(1,128)} %bitcast.2, ...), custom_call_target="tpu_custom_call" | custom-call | tf_op jit(solution)/shard_map/sticks/pallas_call | solution.py:416
  1.4 5.1 %collective-permute-start = (bf16[56,512]{1,0:T(8,128)(2,1)S(1)}, bf16[56,512]{1,0:T(8,128)(2,1)S(1)}, u32[]{:S(2)}, u32[]{:S(2)}) collective-permute-start(bf16[56,512]{1,0:T(8,128)(2,1)S(1)} %get-tuple-element.23), channel_id=1, source_target_pairs={{0,12},{4,8},{8,4},{12,0},{1,13},{5,9},{9,5},{13,1},{2,14},{6,10},... | collective-permute-start | bytes 172040 | tf_op jit(solution)/shard_map/send3/ppermute | solution.py:325
  6.5 0.0 collective-permute-start.1
  6.6 0.6 %collective-permute-start.2 = (bf16[56,512]{1,0:T(8,128)(2,1)S(1)}, bf16[56,512]{1,0:T(8,128)(2,1)S(1)}, u32[]{:S(2)}, u32[]{:S(2)}) collective-permute-start(bf16[56,512]{1,0:T(8,128)(2,1)S(1)} %get-tuple-element.25), channel_id=1, source_target_pairs={{0,4},{4,0},{8,12},{12,8},{1,5},{5,1},{9,13},{13,9},{2,6},{6,2},{1... | collective-permute-start | bytes 172040 | tf_op jit(solution)/shard_map/send1/ppermute | solution.py:325
  7.2 2.9 %preload.1 = (f32[24,192,192]{2,1,0:T(8,128)S(1)}, bf16[384,192]{1,0:T(8,128)(2,1)S(1)}, bf16[2,2,256,256]{3,2,1,0:T(8,128)(2,1)S(1)}, bf16[2,2,256,256]{3,2,1,0...) custom-call(s32[1,192]{1,0:T(1,128)} %bitcast.3, ...), custom_call_target="tpu_custom_call" | custom-call | tf_op jit(solution)/shard_map/preload/pallas_call | solution.py:354
  10.1 0.0 collective-permute-done.refs_1_
  10.1 1.6 %collective-permute-done.1.refs_2_ = bf16[56,512]{1,0:T(8,128)(2,1)S(1)} collective-permute-done((bf16[56,512]{1,0:T(8,128)(2,1)S(1)}, bf16[56,512]{1,0:T(8,128)(2,1)S(1)}, u32[]{:S(2)}, u32[]{:S(2)}) %collective-permute-start.1) | collective-permute-done | bytes 57376 | tf_op jit(solution)/shard_map/send2/ppermute | solution.py:325
  11.6 0.0 collective-permute-done.2.refs_3_
  11.6 10.3 %planes.1 = (bf16[48,512]{1,0:T(8,128)(2,1)S(1)}, bf16[48,512]{1,0:T(8,128)(2,1)S(1)}, bf16[48,512]{1,0:T(8,128)(2,1)S(1)}, bf16[48,512]{1,0:T(8,128)(2,1)S(1)}) custom-call(bf16[56,512]{1,0:T(8,128)(2,1)S(1)} %get-tuple-element.22.refs_0_, bf16[56,512]{1,0:T(8,128)(2,1)S(1)} %collective-permute-done.refs_1_, ...), custom_call_target="tpu_custom_call" | custom-call | tf_op jit(solution)/shard_map/planes/pallas_call | solution.py:384
  22.0 2.7 %collective-permute-start.3 = (bf16[48,512]{1,0:T(8,128)(2,1)S(1)}, bf16[48,512]{1,0:T(8,128)(2,1)S(1)}, u32[]{:S(2)}, u32[]{:S(2)}) collective-permute-start(bf16[48,512]{1,0:T(8,128)(2,1)S(1)} %get-tuple-element.32), channel_id=1, source_target_pairs={{12,0},{8,4},{4,8},{0,12},{13,1},{9,5},{5,9},{1,13},{14,2},{10,6},... | collective-permute-start | bytes 147464 | tf_op jit(solution)/shard_map/back3/ppermute | solution.py:325
  24.7 0.0 collective-permute-start.4
  24.7 1.8 %collective-permute-start.5 = (bf16[48,512]{1,0:T(8,128)(2,1)S(1)}, bf16[48,512]{1,0:T(8,128)(2,1)S(1)}, u32[]{:S(2)}, u32[]{:S(2)}) collective-permute-start(bf16[48,512]{1,0:T(8,128)(2,1)S(1)} %get-tuple-element.34), channel_id=1, source_target_pairs={{4,0},{0,4},{12,8},{8,12},{5,1},{1,5},{13,9},{9,13},{6,2},{2,6},{1... | collective-permute-start | bytes 147464 | tf_op jit(solution)/shard_map/back1/ppermute | solution.py:325
  26.4 1.7 %collective-permute-done.3.refs_1_ = bf16[48,512]{1,0:T(8,128)(2,1)S(1)} collective-permute-done((bf16[48,512]{1,0:T(8,128)(2,1)S(1)}, bf16[48,512]{1,0:T(8,128)(2,1)S(1)}, u32[]{:S(2)}, u32[]{:S(2)}) %collective-permute-start.3) | collective-permute-done | bytes 49184 | tf_op jit(solution)/shard_map/back3/ppermute | solution.py:325
  28.1 1.6 %collective-permute-done.4.refs_2_ = bf16[48,512]{1,0:T(8,128)(2,1)S(1)} collective-permute-done((bf16[48,512]{1,0:T(8,128)(2,1)S(1)}, bf16[48,512]{1,0:T(8,128)(2,1)S(1)}, u32[]{:S(2)}, u32[]{:S(2)}) %collective-permute-start.4) | collective-permute-done | bytes 49184 | tf_op jit(solution)/shard_map/back2/ppermute | solution.py:325
  29.7 0.0 collective-permute-done.5.refs_3_
  29.7 0.9 %columns.1 = f32[1,2,128,256]{3,2,1,0:T(8,128)} custom-call(s32[1]{0:T(128)} %bitcast.me, s32[8,256]{1,0:T(8,128)S(1)} %get-tuple-element.20.half_len, bf16[256,192]{1,0:T(8,128)(2,1)S(1)} %get-tuple-element.21.table, bf16[48,512]{1,0:T(8,128)(2,1)S(1)} %get-tuple-element.31.refs_0_, bf16[48,512]{1,0:T(8,128)(2,1)S(1)} %collective-permute-done.3.refs_1_, ...), custom_call_target="tpu_custom_call" | custom-call | tf_op jit(solution)/shard_map/columns/pallas_call | solution.py:438
Async XLA Ops:
  1.4 8.7 %collective-permute-start = (bf16[56,512]{1,0:T(8,128)(2,1)S(1)}, bf16[56,512]{1,0:T(8,128)(2,1)S(1)}, u32[]{:S(2)}, u32[]{:S(2)}) collective-permute-start(bf16[56,512]{1,0:T(8,128)(2,1)S(1)} %get-tuple-element.23), channel_id=1, source_target_pairs={{0,12},{4,8},{8,4},{12,0},{1,13},{5,9},{9,5},{13,1},{2,14},{6,10},... | collective-permute-start | bytes 172040 | tf_op jit(solution)/shard_map/send3/ppermute | solution.py:325
  6.5 5.1 %collective-permute-start.1 = (bf16[56,512]{1,0:T(8,128)(2,1)S(1)}, bf16[56,512]{1,0:T(8,128)(2,1)S(1)}, u32[]{:S(2)}, u32[]{:S(2)}) collective-permute-start(bf16[56,512]{1,0:T(8,128)(2,1)S(1)} %get-tuple-element.24), channel_id=1, source_target_pairs={{0,8},{4,12},{8,0},{12,4},{1,9},{5,13},{9,1},{13,5},{2,10},{6,14},... | collective-permute-start | bytes 172040 | tf_op jit(solution)/shard_map/send2/ppermute | solution.py:325
  6.6 5.1 %collective-permute-start.2 = (bf16[56,512]{1,0:T(8,128)(2,1)S(1)}, bf16[56,512]{1,0:T(8,128)(2,1)S(1)}, u32[]{:S(2)}, u32[]{:S(2)}) collective-permute-start(bf16[56,512]{1,0:T(8,128)(2,1)S(1)} %get-tuple-element.25), channel_id=1, source_target_pairs={{0,4},{4,0},{8,12},{12,8},{1,5},{5,1},{9,13},{13,9},{2,6},{6,2},{1... | collective-permute-start | bytes 172040 | tf_op jit(solution)/shard_map/send1/ppermute | solution.py:325
  22.0 6.1 %collective-permute-start.3 = (bf16[48,512]{1,0:T(8,128)(2,1)S(1)}, bf16[48,512]{1,0:T(8,128)(2,1)S(1)}, u32[]{:S(2)}, u32[]{:S(2)}) collective-permute-start(bf16[48,512]{1,0:T(8,128)(2,1)S(1)} %get-tuple-element.32), channel_id=1, source_target_pairs={{12,0},{8,4},{4,8},{0,12},{13,1},{9,5},{5,9},{1,13},{14,2},{10,6},... | collective-permute-start | bytes 147464 | tf_op jit(solution)/shard_map/back3/ppermute | solution.py:325
  24.7 5.0 %collective-permute-start.4 = (bf16[48,512]{1,0:T(8,128)(2,1)S(1)}, bf16[48,512]{1,0:T(8,128)(2,1)S(1)}, u32[]{:S(2)}, u32[]{:S(2)}) collective-permute-start(bf16[48,512]{1,0:T(8,128)(2,1)S(1)} %get-tuple-element.33), channel_id=1, source_target_pairs={{8,0},{12,4},{0,8},{4,12},{9,1},{13,5},{1,9},{5,13},{10,2},{14,6},... | collective-permute-start | bytes 147464 | tf_op jit(solution)/shard_map/back2/ppermute | solution.py:325
  24.7 5.0 %collective-permute-start.5 = (bf16[48,512]{1,0:T(8,128)(2,1)S(1)}, bf16[48,512]{1,0:T(8,128)(2,1)S(1)}, u32[]{:S(2)}, u32[]{:S(2)}) collective-permute-start(bf16[48,512]{1,0:T(8,128)(2,1)S(1)} %get-tuple-element.34), channel_id=1, source_target_pairs={{4,0},{0,4},{12,8},{8,12},{5,1},{1,5},{13,9},{9,13},{6,2},{2,6},{1... | collective-permute-start | bytes 147464 | tf_op jit(solution)/shard_map/back1/ppermute | solution.py:325

commit v7 on v6

--- a/solution.py
+++ b/solution.py
@@ -13,8 +13,11 @@
 BF16 = jnp.bfloat16
 PARAMS = pltpu.CompilerParams(vmem_limit_bytes=28 << 20)
 IN_SMEM = pl.BlockSpec(memory_space=pltpu.SMEM)
+PLANE_PARAMS = PARAMS
 IN_HBM = pl.BlockSpec(memory_space=pltpu.HBM)
 IN_VMEM = pl.BlockSpec(memory_space=pltpu.VMEM)
+LAG = 6
+TILE = 256
 GROUPS = (24, 16, 12, 8, 4, 2)
 
 
@@ -232,9 +235,11 @@
                 parts.append(jnp.concatenate(lanes, 1))
             return jnp.concatenate(parts, 0)
 
-        def along_x(bundle, grid):
+        def fields_of(bundle):
+            return jnp.concatenate([pot[plane] for pair in bundle for plane, _ in pair], 1)
+
+        def along_x(grid, field):
             fields = mm(fwd_x[...], grid)
-            field = jnp.concatenate([pot[plane] for pair in bundle for plane, _ in pair], 1)
             return [
                 (fields[comp * grid_side : (comp + 1) * grid_side] * field).astype(BF16)
                 for comp in range(2)
@@ -242,6 +247,26 @@
 
         def back_x(product):
             return (mm(inv_x[0], product[0]) + mm(inv_x[1], product[1])).astype(BF16)
+
+        def both_x(bundles, grids):
+            tiles = []
+            for bundle, grid in zip(bundles, grids):
+                field = fields_of(bundle)
+                for start in range(0, grid.shape[1], TILE):
+                    lanes = slice(start, min(start + TILE, grid.shape[1]))
+                    tiles.append((grid[:, lanes], field[:, lanes]))
+            products, parts = [], []
+            for turn in range(len(tiles) + LAG):
+                if turn < len(tiles):
+                    products.append(along_x(*tiles[turn]))
+                if turn >= LAG:
+                    parts.append(back_x(products[turn - LAG]))
+            result = []
+            for grid in grids:
+                count = -(-grid.shape[1] // TILE)
+                result.append(jnp.concatenate(parts[:count], 1))
+                parts = parts[count:]
+            return result
 
         def back_y(grid, count):
             result = []
@@ -264,17 +289,19 @@
                 bottom = grid[i * half + quarter : (i + 1) * half]
                 for lanes in (slice(0, lane_pad), slice(lane_pad, 2 * lane_pad)):
                     stacked.append(jnp.concatenate([top[:, lanes], bottom[:, lanes]], 1))
-            found = mm(jnp.concatenate(stacked, 0), high[...])
-            for i, (plane, band) in enumerate(units):
-                for comp in range(2):
-                    start = i * half + comp * quarter
-                    line = jnp.sum(found[start : start + quarter] * low[...], axis=0, keepdims=True)
-                    acc[pl.ds((band * 2 + comp) * share + base + plane, 1), :] = line
+            stacked = jnp.concatenate(stacked, 0)
+            for start in range(0, high.shape[1], TILE):
+                lanes = slice(start, min(start + TILE, high.shape[1]))
+                found = mm(stacked, high[:, lanes])
+                for i, (plane, band) in enumerate(units):
+                    for comp in range(2):
+                        top = i * half + comp * quarter
+                        line = jnp.sum(found[top : top + quarter] * low[:, lanes], axis=0, keepdims=True)
+                        acc[pl.ds((band * 2 + comp) * share + base + plane, 1), lanes] = line
 
         grids = [[spread(units) for units in by_phase(bundle)] for bundle in bundles]
         grids = [along_y(grid) for grid in grids]
-        products = [along_x(bundle, grid) for bundle, grid in zip(bundles, grids)]
-        grids = [back_x(product) for product in products]
+        grids = both_x(bundles, grids)
         grids = [back_y(grid, len(bundle)) for bundle, grid in zip(bundles, grids)]
         for bundle, grid in zip(bundles, grids):
             for units, part in zip(by_phase(bundle), grid):
@@ -397,7 +424,7 @@
             pltpu.VMEM((later, group, grid_side, grid_side), F32),
             pltpu.SemaphoreType.DMA((later,)),
         ],
-        compiler_params=PARAMS,
+        compiler_params=PLANE_PARAMS,
         name="planes",
     )(*received, *stay(potential), pot_first, *tables)
 

time: 30.8 us -> 30.4 us (0.987)
    pallas_call x1, Pallas kernels: 10.3 us -> 9.98 us  [plane_call(): pl.pallas_call(functools.partial(plane_kernel, sources=owners, bands=band...]
where the time goes in v7:
time: 30.4 us; the launch traced here: 30.2 us
  Pallas kernels  15.2 us (50%)
  starting transfers between devices  10.2 us (34%)
  waiting for transfers between devices  4.79 us (16%)
    ppermute x6, starting transfers between devices, exchange(): result.append(lax.ppermute(part, 'fft', pairs))  10.2 us
    pallas_call x1, Pallas kernels, plane_call(): pl.pallas_call(functools.partial(plane_kernel, sources=owners, bands=band...  9.98 us
    ppermute x6, waiting for transfers between devices, exchange(): result.append(lax.ppermute(part, 'fft', pairs))  4.79 us
    pallas_call x1, Pallas kernels, preload(): pl.pallas_call(preload_kernel, in_specs=[IN_HBM] * (len(arrays) + 3), out...  2.86 us
    pallas_call x1, Pallas kernels, body(): pl.pallas_call(functools.partial(stick_kernel, owners=owners, share=share...  1.4 us
    pallas_call x1, Pallas kernels, body(): pl.pallas_call(functools.partial(column_kernel, owners=owners, slots=slot...  0.94 us
  transfers between devices with their start and end apart: 6, of which 3 were waited for; matrix products, arithmetic and copies ran while one was open for 0% of the time, Pallas kernels for 9%

profile of v7, /device:TPU:0, one launch (start us, length us, event | category | flops | bytes accessed | tf_op | source)
XLA Modules:
  0.0 30.2 jit_solution(962914773599172696)
XLA Ops:
  0.0 1.4 %sticks.1 = (bf16[56,512]{1,0:T(8,128)(2,1)S(1)}, bf16[56,512]{1,0:T(8,128)(2,1)S(1)}, bf16[56,512]{1,0:T(8,128)(2,1)S(1)}, bf16[56,512]{1,0:T(8,128)(2,1)S(1)}) custom-call(s32[1]{0:T(128)} %bitcast.me, bf16[1,2,128,256]{3,2,1,0:T(8,128)(2,1)} %coeff_h.1, s32[3,256]{1,0:T(4,128)} %smap_h.3, s32[1,192]{1,0:T(1,128)} %bitcast.2, ...), custom_call_target="tpu_custom_call" | custom-call | tf_op jit(solution)/shard_map/sticks/pallas_call | solution.py:443
  1.4 5.1 %collective-permute-start = (bf16[56,512]{1,0:T(8,128)(2,1)S(1)}, bf16[56,512]{1,0:T(8,128)(2,1)S(1)}, u32[]{:S(2)}, u32[]{:S(2)}) collective-permute-start(bf16[56,512]{1,0:T(8,128)(2,1)S(1)} %get-tuple-element.23), channel_id=1, source_target_pairs={{0,12},{4,8},{8,4},{12,0},{1,13},{5,9},{9,5},{13,1},{2,14},{6,10},... | collective-permute-start | bytes 172040 | tf_op jit(solution)/shard_map/send3/ppermute | solution.py:352
  6.5 0.0 collective-permute-start.1
  6.6 0.6 %collective-permute-start.2 = (bf16[56,512]{1,0:T(8,128)(2,1)S(1)}, bf16[56,512]{1,0:T(8,128)(2,1)S(1)}, u32[]{:S(2)}, u32[]{:S(2)}) collective-permute-start(bf16[56,512]{1,0:T(8,128)(2,1)S(1)} %get-tuple-element.25), channel_id=1, source_target_pairs={{0,4},{4,0},{8,12},{12,8},{1,5},{5,1},{9,13},{13,9},{2,6},{6,2},{1... | collective-permute-start | bytes 172040 | tf_op jit(solution)/shard_map/send1/ppermute | solution.py:352
  7.2 2.9 %preload.1 = (f32[24,192,192]{2,1,0:T(8,128)S(1)}, bf16[384,192]{1,0:T(8,128)(2,1)S(1)}, bf16[2,2,256,256]{3,2,1,0:T(8,128)(2,1)S(1)}, bf16[2,2,256,256]{3,2,1,0...) custom-call(s32[1,192]{1,0:T(1,128)} %bitcast.3, ...), custom_call_target="tpu_custom_call" | custom-call | tf_op jit(solution)/shard_map/preload/pallas_call | solution.py:381
  10.1 0.0 collective-permute-done.refs_1_
  10.1 1.6 %collective-permute-done.1.refs_2_ = bf16[56,512]{1,0:T(8,128)(2,1)S(1)} collective-permute-done((bf16[56,512]{1,0:T(8,128)(2,1)S(1)}, bf16[56,512]{1,0:T(8,128)(2,1)S(1)}, u32[]{:S(2)}, u32[]{:S(2)}) %collective-permute-start.1) | collective-permute-done | bytes 57376 | tf_op jit(solution)/shard_map/send2/ppermute | solution.py:352
  11.6 0.0 collective-permute-done.2.refs_3_
  11.6 10.0 %planes.1 = (bf16[48,512]{1,0:T(8,128)(2,1)S(1)}, bf16[48,512]{1,0:T(8,128)(2,1)S(1)}, bf16[48,512]{1,0:T(8,128)(2,1)S(1)}, bf16[48,512]{1,0:T(8,128)(2,1)S(1)}) custom-call(bf16[56,512]{1,0:T(8,128)(2,1)S(1)} %get-tuple-element.22.refs_0_, bf16[56,512]{1,0:T(8,128)(2,1)S(1)} %collective-permute-done.refs_1_, ...), custom_call_target="tpu_custom_call" | custom-call | tf_op jit(solution)/shard_map/planes/pallas_call | solution.py:411
  21.6 2.7 %collective-permute-start.3 = (bf16[48,512]{1,0:T(8,128)(2,1)S(1)}, bf16[48,512]{1,0:T(8,128)(2,1)S(1)}, u32[]{:S(2)}, u32[]{:S(2)}) collective-permute-start(bf16[48,512]{1,0:T(8,128)(2,1)S(1)} %get-tuple-element.32), channel_id=1, source_target_pairs={{12,0},{8,4},{4,8},{0,12},{13,1},{9,5},{5,9},{1,13},{14,2},{10,6},... | collective-permute-start | bytes 147464 | tf_op jit(solution)/shard_map/back3/ppermute | solution.py:352
  24.3 0.0 collective-permute-start.4
  24.3 1.8 %collective-permute-start.5 = (bf16[48,512]{1,0:T(8,128)(2,1)S(1)}, bf16[48,512]{1,0:T(8,128)(2,1)S(1)}, u32[]{:S(2)}, u32[]{:S(2)}) collective-permute-start(bf16[48,512]{1,0:T(8,128)(2,1)S(1)} %get-tuple-element.34), channel_id=1, source_target_pairs={{4,0},{0,4},{12,8},{8,12},{5,1},{1,5},{13,9},{9,13},{6,2},{2,6},{1... | collective-permute-start | bytes 147464 | tf_op jit(solution)/shard_map/back1/ppermute | solution.py:352
  26.1 1.7 %collective-permute-done.3.refs_1_ = bf16[48,512]{1,0:T(8,128)(2,1)S(1)} collective-permute-done((bf16[48,512]{1,0:T(8,128)(2,1)S(1)}, bf16[48,512]{1,0:T(8,128)(2,1)S(1)}, u32[]{:S(2)}, u32[]{:S(2)}) %collective-permute-start.3) | collective-permute-done | bytes 49184 | tf_op jit(solution)/shard_map/back3/ppermute | solution.py:352
  27.8 1.6 %collective-permute-done.4.refs_2_ = bf16[48,512]{1,0:T(8,128)(2,1)S(1)} collective-permute-done((bf16[48,512]{1,0:T(8,128)(2,1)S(1)}, bf16[48,512]{1,0:T(8,128)(2,1)S(1)}, u32[]{:S(2)}, u32[]{:S(2)}) %collective-permute-start.4) | collective-permute-done | bytes 49184 | tf_op jit(solution)/shard_map/back2/ppermute | solution.py:352
  29.3 0.0 collective-permute-done.5.refs_3_
  29.3 0.9 %columns.1 = f32[1,2,128,256]{3,2,1,0:T(8,128)} custom-call(s32[1]{0:T(128)} %bitcast.me, s32[8,256]{1,0:T(8,128)S(1)} %get-tuple-element.20.half_len, bf16[256,192]{1,0:T(8,128)(2,1)S(1)} %get-tuple-element.21.table, bf16[48,512]{1,0:T(8,128)(2,1)S(1)} %get-tuple-element.31.refs_0_, bf16[48,512]{1,0:T(8,128)(2,1)S(1)} %collective-permute-done.3.refs_1_, ...), custom_call_target="tpu_custom_call" | custom-call | tf_op jit(solution)/shard_map/columns/pallas_call | solution.py:465
Async XLA Ops:
  1.4 8.7 %collective-permute-start = (bf16[56,512]{1,0:T(8,128)(2,1)S(1)}, bf16[56,512]{1,0:T(8,128)(2,1)S(1)}, u32[]{:S(2)}, u32[]{:S(2)}) collective-permute-start(bf16[56,512]{1,0:T(8,128)(2,1)S(1)} %get-tuple-element.23), channel_id=1, source_target_pairs={{0,12},{4,8},{8,4},{12,0},{1,13},{5,9},{9,5},{13,1},{2,14},{6,10},... | collective-permute-start | bytes 172040 | tf_op jit(solution)/shard_map/send3/ppermute | solution.py:352
  6.5 5.1 %collective-permute-start.1 = (bf16[56,512]{1,0:T(8,128)(2,1)S(1)}, bf16[56,512]{1,0:T(8,128)(2,1)S(1)}, u32[]{:S(2)}, u32[]{:S(2)}) collective-permute-start(bf16[56,512]{1,0:T(8,128)(2,1)S(1)} %get-tuple-element.24), channel_id=1, source_target_pairs={{0,8},{4,12},{8,0},{12,4},{1,9},{5,13},{9,1},{13,5},{2,10},{6,14},... | collective-permute-start | bytes 172040 | tf_op jit(solution)/shard_map/send2/ppermute | solution.py:352
  6.6 5.1 %collective-permute-start.2 = (bf16[56,512]{1,0:T(8,128)(2,1)S(1)}, bf16[56,512]{1,0:T(8,128)(2,1)S(1)}, u32[]{:S(2)}, u32[]{:S(2)}) collective-permute-start(bf16[56,512]{1,0:T(8,128)(2,1)S(1)} %get-tuple-element.25), channel_id=1, source_target_pairs={{0,4},{4,0},{8,12},{12,8},{1,5},{5,1},{9,13},{13,9},{2,6},{6,2},{1... | collective-permute-start | bytes 172040 | tf_op jit(solution)/shard_map/send1/ppermute | solution.py:352
  21.6 6.1 %collective-permute-start.3 = (bf16[48,512]{1,0:T(8,128)(2,1)S(1)}, bf16[48,512]{1,0:T(8,128)(2,1)S(1)}, u32[]{:S(2)}, u32[]{:S(2)}) collective-permute-start(bf16[48,512]{1,0:T(8,128)(2,1)S(1)} %get-tuple-element.32), channel_id=1, source_target_pairs={{12,0},{8,4},{4,8},{0,12},{13,1},{9,5},{5,9},{1,13},{14,2},{10,6},... | collective-permute-start | bytes 147464 | tf_op jit(solution)/shard_map/back3/ppermute | solution.py:352
  24.3 5.0 %collective-permute-start.4 = (bf16[48,512]{1,0:T(8,128)(2,1)S(1)}, bf16[48,512]{1,0:T(8,128)(2,1)S(1)}, u32[]{:S(2)}, u32[]{:S(2)}) collective-permute-start(bf16[48,512]{1,0:T(8,128)(2,1)S(1)} %get-tuple-element.33), channel_id=1, source_target_pairs={{8,0},{12,4},{0,8},{4,12},{9,1},{13,5},{1,9},{5,13},{10,2},{14,6},... | collective-permute-start | bytes 147464 | tf_op jit(solution)/shard_map/back2/ppermute | solution.py:352
  24.3 5.0 %collective-permute-start.5 = (bf16[48,512]{1,0:T(8,128)(2,1)S(1)}, bf16[48,512]{1,0:T(8,128)(2,1)S(1)}, u32[]{:S(2)}, u32[]{:S(2)}) collective-permute-start(bf16[48,512]{1,0:T(8,128)(2,1)S(1)} %get-tuple-element.34), channel_id=1, source_target_pairs={{4,0},{0,4},{12,8},{8,12},{5,1},{1,5},{13,9},{9,13},{6,2},{2,6},{1... | collective-permute-start | bytes 147464 | tf_op jit(solution)/shard_map/back1/ppermute | solution.py:352

commit v8 on v7

--- a/solution.py
+++ b/solution.py
@@ -301,16 +301,24 @@
 
         grids = [[spread(units) for units in by_phase(bundle)] for bundle in bundles]
         grids = [along_y(grid) for grid in grids]
+        yield
         grids = both_x(bundles, grids)
         grids = [back_y(grid, len(bundle)) for bundle, grid in zip(bundles, grids)]
+        yield
         for bundle, grid in zip(bundles, grids):
             for units, part in zip(by_phase(bundle), grid):
                 pick(units, part)
-
+        yield
+
+    groups = [one_group(step) for step in range(steps)]
+    next(groups[0])
     for step in range(steps):
         if step > 0:
             pot_copy(step).wait()
-        one_group(step)
+        next(groups[step])
+        if step + 1 < steps:
+            next(groups[step + 1])
+        next(groups[step])
 
     spread_out = mm(acc[...].astype(BF16), select[...]).astype(BF16)
     for src in range(sources):

time: 30.4 us -> 30.4 us (level)
  no operation moved by 1% of the time
where the time goes in v8:
time: 30.4 us; the launch traced here: 30.2 us
  Pallas kernels  15.2 us (50%)
  starting transfers between devices  10.2 us (34%)
  waiting for transfers between devices  4.8 us (16%)
    ppermute x6, starting transfers between devices, exchange(): result.append(lax.ppermute(part, 'fft', pairs))  10.2 us
    pallas_call x1, Pallas kernels, plane_call(): pl.pallas_call(functools.partial(plane_kernel, sources=owners, bands=band...  9.96 us
    ppermute x6, waiting for transfers between devices, exchange(): result.append(lax.ppermute(part, 'fft', pairs))  4.8 us
    pallas_call x1, Pallas kernels, preload(): pl.pallas_call(preload_kernel, in_specs=[IN_HBM] * (len(arrays) + 3), out...  2.86 us
    pallas_call x1, Pallas kernels, body(): pl.pallas_call(functools.partial(stick_kernel, owners=owners, share=share...  1.4 us
    pallas_call x1, Pallas kernels, body(): pl.pallas_call(functools.partial(column_kernel, owners=owners, slots=slot...  0.94 us
  transfers between devices with their start and end apart: 6, of which 3 were waited for; matrix products, arithmetic and copies ran while one was open for 0% of the time, Pallas kernels for 9%

profile of v8, /device:TPU:0, one launch (start us, length us, event | category | flops | bytes accessed | tf_op | source)
XLA Modules:
  0.0 30.2 jit_solution(16485179540265996997)
XLA Ops:
  0.0 1.4 %sticks.1 = (bf16[56,512]{1,0:T(8,128)(2,1)S(1)}, bf16[56,512]{1,0:T(8,128)(2,1)S(1)}, bf16[56,512]{1,0:T(8,128)(2,1)S(1)}, bf16[56,512]{1,0:T(8,128)(2,1)S(1)}) custom-call(s32[1]{0:T(128)} %bitcast.me, bf16[1,2,128,256]{3,2,1,0:T(8,128)(2,1)} %coeff_h.1, s32[3,256]{1,0:T(4,128)} %smap_h.3, s32[1,192]{1,0:T(1,128)} %bitcast.2, ...), custom_call_target="tpu_custom_call" | custom-call | tf_op jit(solution)/shard_map/sticks/pallas_call | solution.py:451
  1.4 5.1 %collective-permute-start = (bf16[56,512]{1,0:T(8,128)(2,1)S(1)}, bf16[56,512]{1,0:T(8,128)(2,1)S(1)}, u32[]{:S(2)}, u32[]{:S(2)}) collective-permute-start(bf16[56,512]{1,0:T(8,128)(2,1)S(1)} %get-tuple-element.23), channel_id=1, source_target_pairs={{0,12},{4,8},{8,4},{12,0},{1,13},{5,9},{9,5},{13,1},{2,14},{6,10},... | collective-permute-start | bytes 172040 | tf_op jit(solution)/shard_map/send3/ppermute | solution.py:360
  6.5 0.0 collective-permute-start.1
  6.6 0.6 %collective-permute-start.2 = (bf16[56,512]{1,0:T(8,128)(2,1)S(1)}, bf16[56,512]{1,0:T(8,128)(2,1)S(1)}, u32[]{:S(2)}, u32[]{:S(2)}) collective-permute-start(bf16[56,512]{1,0:T(8,128)(2,1)S(1)} %get-tuple-element.25), channel_id=1, source_target_pairs={{0,4},{4,0},{8,12},{12,8},{1,5},{5,1},{9,13},{13,9},{2,6},{6,2},{1... | collective-permute-start | bytes 172040 | tf_op jit(solution)/shard_map/send1/ppermute | solution.py:360
  7.2 2.9 %preload.1 = (f32[24,192,192]{2,1,0:T(8,128)S(1)}, bf16[384,192]{1,0:T(8,128)(2,1)S(1)}, bf16[2,2,256,256]{3,2,1,0:T(8,128)(2,1)S(1)}, bf16[2,2,256,256]{3,2,1,0...) custom-call(s32[1,192]{1,0:T(1,128)} %bitcast.3, ...), custom_call_target="tpu_custom_call" | custom-call | tf_op jit(solution)/shard_map/preload/pallas_call | solution.py:389
  10.1 0.0 collective-permute-done.refs_1_
  10.1 1.6 %collective-permute-done.1.refs_2_ = bf16[56,512]{1,0:T(8,128)(2,1)S(1)} collective-permute-done((bf16[56,512]{1,0:T(8,128)(2,1)S(1)}, bf16[56,512]{1,0:T(8,128)(2,1)S(1)}, u32[]{:S(2)}, u32[]{:S(2)}) %collective-permute-start.1) | collective-permute-done | bytes 57376 | tf_op jit(solution)/shard_map/send2/ppermute | solution.py:360
  11.6 0.0 collective-permute-done.2.refs_3_
  11.6 10.0 %planes.1 = (bf16[48,512]{1,0:T(8,128)(2,1)S(1)}, bf16[48,512]{1,0:T(8,128)(2,1)S(1)}, bf16[48,512]{1,0:T(8,128)(2,1)S(1)}, bf16[48,512]{1,0:T(8,128)(2,1)S(1)}) custom-call(bf16[56,512]{1,0:T(8,128)(2,1)S(1)} %get-tuple-element.22.refs_0_, bf16[56,512]{1,0:T(8,128)(2,1)S(1)} %collective-permute-done.refs_1_, ...), custom_call_target="tpu_custom_call" | custom-call | tf_op jit(solution)/shard_map/planes/pallas_call | solution.py:419
  21.6 2.7 %collective-permute-start.3 = (bf16[48,512]{1,0:T(8,128)(2,1)S(1)}, bf16[48,512]{1,0:T(8,128)(2,1)S(1)}, u32[]{:S(2)}, u32[]{:S(2)}) collective-permute-start(bf16[48,512]{1,0:T(8,128)(2,1)S(1)} %get-tuple-element.32), channel_id=1, source_target_pairs={{12,0},{8,4},{4,8},{0,12},{13,1},{9,5},{5,9},{1,13},{14,2},{10,6},... | collective-permute-start | bytes 147464 | tf_op jit(solution)/shard_map/back3/ppermute | solution.py:360
  24.3 0.0 collective-permute-start.4
  24.3 1.8 %collective-permute-start.5 = (bf16[48,512]{1,0:T(8,128)(2,1)S(1)}, bf16[48,512]{1,0:T(8,128)(2,1)S(1)}, u32[]{:S(2)}, u32[]{:S(2)}) collective-permute-start(bf16[48,512]{1,0:T(8,128)(2,1)S(1)} %get-tuple-element.34), channel_id=1, source_target_pairs={{4,0},{0,4},{12,8},{8,12},{5,1},{1,5},{13,9},{9,13},{6,2},{2,6},{1... | collective-permute-start | bytes 147464 | tf_op jit(solution)/shard_map/back1/ppermute | solution.py:360
  26.1 1.7 %collective-permute-done.3.refs_1_ = bf16[48,512]{1,0:T(8,128)(2,1)S(1)} collective-permute-done((bf16[48,512]{1,0:T(8,128)(2,1)S(1)}, bf16[48,512]{1,0:T(8,128)(2,1)S(1)}, u32[]{:S(2)}, u32[]{:S(2)}) %collective-permute-start.3) | collective-permute-done | bytes 49184 | tf_op jit(solution)/shard_map/back3/ppermute | solution.py:360
  27.7 1.6 %collective-permute-done.4.refs_2_ = bf16[48,512]{1,0:T(8,128)(2,1)S(1)} collective-permute-done((bf16[48,512]{1,0:T(8,128)(2,1)S(1)}, bf16[48,512]{1,0:T(8,128)(2,1)S(1)}, u32[]{:S(2)}, u32[]{:S(2)}) %collective-permute-start.4) | collective-permute-done | bytes 49184 | tf_op jit(solution)/shard_map/back2/ppermute | solution.py:360
  29.3 0.0 collective-permute-done.5.refs_3_
  29.3 0.9 %columns.1 = f32[1,2,128,256]{3,2,1,0:T(8,128)} custom-call(s32[1]{0:T(128)} %bitcast.me, s32[8,256]{1,0:T(8,128)S(1)} %get-tuple-element.20.half_len, bf16[256,192]{1,0:T(8,128)(2,1)S(1)} %get-tuple-element.21.table, bf16[48,512]{1,0:T(8,128)(2,1)S(1)} %get-tuple-element.31.refs_0_, bf16[48,512]{1,0:T(8,128)(2,1)S(1)} %collective-permute-done.3.refs_1_, ...), custom_call_target="tpu_custom_call" | custom-call | tf_op jit(solution)/shard_map/columns/pallas_call | solution.py:473
Async XLA Ops:
  1.4 8.7 %collective-permute-start = (bf16[56,512]{1,0:T(8,128)(2,1)S(1)}, bf16[56,512]{1,0:T(8,128)(2,1)S(1)}, u32[]{:S(2)}, u32[]{:S(2)}) collective-permute-start(bf16[56,512]{1,0:T(8,128)(2,1)S(1)} %get-tuple-element.23), channel_id=1, source_target_pairs={{0,12},{4,8},{8,4},{12,0},{1,13},{5,9},{9,5},{13,1},{2,14},{6,10},... | collective-permute-start | bytes 172040 | tf_op jit(solution)/shard_map/send3/ppermute | solution.py:360
  6.5 5.1 %collective-permute-start.1 = (bf16[56,512]{1,0:T(8,128)(2,1)S(1)}, bf16[56,512]{1,0:T(8,128)(2,1)S(1)}, u32[]{:S(2)}, u32[]{:S(2)}) collective-permute-start(bf16[56,512]{1,0:T(8,128)(2,1)S(1)} %get-tuple-element.24), channel_id=1, source_target_pairs={{0,8},{4,12},{8,0},{12,4},{1,9},{5,13},{9,1},{13,5},{2,10},{6,14},... | collective-permute-start | bytes 172040 | tf_op jit(solution)/shard_map/send2/ppermute | solution.py:360
  6.6 5.1 %collective-permute-start.2 = (bf16[56,512]{1,0:T(8,128)(2,1)S(1)}, bf16[56,512]{1,0:T(8,128)(2,1)S(1)}, u32[]{:S(2)}, u32[]{:S(2)}) collective-permute-start(bf16[56,512]{1,0:T(8,128)(2,1)S(1)} %get-tuple-element.25), channel_id=1, source_target_pairs={{0,4},{4,0},{8,12},{12,8},{1,5},{5,1},{9,13},{13,9},{2,6},{6,2},{1... | collective-permute-start | bytes 172040 | tf_op jit(solution)/shard_map/send1/ppermute | solution.py:360
  21.6 6.1 %collective-permute-start.3 = (bf16[48,512]{1,0:T(8,128)(2,1)S(1)}, bf16[48,512]{1,0:T(8,128)(2,1)S(1)}, u32[]{:S(2)}, u32[]{:S(2)}) collective-permute-start(bf16[48,512]{1,0:T(8,128)(2,1)S(1)} %get-tuple-element.32), channel_id=1, source_target_pairs={{12,0},{8,4},{4,8},{0,12},{13,1},{9,5},{5,9},{1,13},{14,2},{10,6},... | collective-permute-start | bytes 147464 | tf_op jit(solution)/shard_map/back3/ppermute | solution.py:360
  24.3 5.0 %collective-permute-start.4 = (bf16[48,512]{1,0:T(8,128)(2,1)S(1)}, bf16[48,512]{1,0:T(8,128)(2,1)S(1)}, u32[]{:S(2)}, u32[]{:S(2)}) collective-permute-start(bf16[48,512]{1,0:T(8,128)(2,1)S(1)} %get-tuple-element.33), channel_id=1, source_target_pairs={{8,0},{12,4},{0,8},{4,12},{9,1},{13,5},{1,9},{5,13},{10,2},{14,6},... | collective-permute-start | bytes 147464 | tf_op jit(solution)/shard_map/back2/ppermute | solution.py:360
  24.3 5.0 %collective-permute-start.5 = (bf16[48,512]{1,0:T(8,128)(2,1)S(1)}, bf16[48,512]{1,0:T(8,128)(2,1)S(1)}, u32[]{:S(2)}, u32[]{:S(2)}) collective-permute-start(bf16[48,512]{1,0:T(8,128)(2,1)S(1)} %get-tuple-element.34), channel_id=1, source_target_pairs={{4,0},{0,4},{12,8},{8,12},{5,1},{1,5},{13,9},{9,13},{6,2},{2,6},{1... | collective-permute-start | bytes 147464 | tf_op jit(solution)/shard_map/back1/ppermute | solution.py:360
